TPU v7x, 16 devices: a whole 2x2x2 slice. The times are simulated.
16 devices in a mesh: tp: 2 (over z), dp: 8 (over y, x, core).
Axes of the slice: x: 2, y: 2, z: 2, core: 2. Of those that a mesh axis runs over, the one named last changes fastest.
Arguments:
- design: float32 [65536, 2048], P('dp', 'tp')
- target: float32 [65536], P('dp')
- ridge: float32 [], replicated
Outputs:
- output 1: float32 [2048], replicated
- output 2: float32 [65536], P('dp')
All inputs are finite; a program needn't handle non-finite values.
Results may differ from a plain program's by a relative error of at most 0.001.
Values sent between devices are 32-bit elements.
A program may use at most 1 GiB of HBM per device.

v0:
```python
import jax
import jax.numpy as jnp
from jax import lax
from jax.sharding import PartitionSpec as P

HIGHEST = lax.Precision.HIGHEST
CONTRACT_ROWS = (((0,), (0,)), ((), ()))


def solve_factored(chol_low, rhs_vec):
    half_solve = lax.linalg.triangular_solve(chol_low, rhs_vec[:, None], left_side=True, lower=True)
    return lax.linalg.triangular_solve(chol_low, half_solve, left_side=True, lower=True, transpose_a=True)[:, 0]


def solution(mesh):
    col_ways = mesh.shape['tp']

    def local_fit(design_blk, target_blk, ridge):
        rows_dev, cols_dev = design_blk.shape
        features = cols_dev * col_ways
        sub_rows = rows_dev // col_ways
        col_index = lax.axis_index('tp')
        row_panel = lax.all_to_all(design_blk, 'tp', 0, 1, tiled=True)
        target_part = lax.dynamic_slice_in_dim(target_blk, col_index * sub_rows, sub_rows)
        gram_part = lax.dot_general(row_panel, row_panel, CONTRACT_ROWS, precision=HIGHEST, preferred_element_type=jnp.float32)
        moment_part = lax.dot_general(row_panel, target_part, CONTRACT_ROWS, precision=HIGHEST, preferred_element_type=jnp.float32)
        gram_mat = lax.psum(gram_part, ('tp', 'dp'))
        moment_vec = lax.psum(moment_part, ('tp', 'dp'))
        chol_low = jnp.linalg.cholesky(gram_mat + ridge * jnp.eye(features, dtype=jnp.float32))
        coeffs = solve_factored(chol_low, moment_vec)
        coeff_blk = lax.dynamic_slice_in_dim(coeffs, col_index * cols_dev, cols_dev)
        part_fit = jnp.dot(design_blk, coeff_blk, precision=HIGHEST, preferred_element_type=jnp.float32)
        fitted = lax.psum(part_fit, 'tp')
        return coeffs, target_blk - fitted

    return jax.shard_map(local_fit, mesh=mesh, in_specs=(P('dp', 'tp'), P('dp'), P()), out_specs=(P(), P('dp')), check_vma=False)
```

profile of v0, /device:TPU:0, one launch (start us, length us, event | category | flops | bytes accessed | tf_op | source)
XLA Modules:
  0.0 1716.5 jit_solution(55955799440125947)
XLA Ops:
  7.2 395.8 %all_to_all.19 = f32[2,4096,1024]{2,1,0:T(8,128)} all-to-all(f32[2,4096,1024]{2,1,0:T(8,128)} %bitcast.736), channel_id=1, replica_groups=mesh['tp'=2,'dp'=8] {'tp'}, dimensions={0} | all-to-all | bytes 67108864 | tf_op jit(solution)/shard_map/all_to_all | solution.py:23
  403.0 31.1 %copy.73 = f32[4096,2,1024]{0,2,1:T(8,128)} copy(f32[4096,2,1024]{2,0,1:T(8,128)} %bitcast.739) | data formatting | bytes 67108864 | tf_op jit(solution)/shard_map/all_to_all | solution.py:23
  434.1 224.4 %fusion.255 = f32[2048,2048]{0,1:T(8,128)} fusion(f32[4096,2048]{0,1:T(8,128)} %bitcast.737), kind=kOutput, calls=%fused_computation.620 | convolution fusion | flops 206158430208 | bytes 50331648 | tf_op jit(solution)/shard_map/dot_general | solution.py:25
  659.3 30.7 %fusion.256 = f32[1,2048]{1,0:T(1,128)S(1)} fusion(f32[4096,1]{0,1:T(1,128)S(1)} %bitcast.741, f32[4096,2048]{0,1:T(8,128)} %bitcast.738), kind=kOutput, calls=%fused_computation.621 | convolution fusion | flops 100663296 | bytes 33579008 | tf_op jit(solution)/shard_map/dot_general | solution.py:26
  690.0 32.6 %psum.22 = f32[2048]{0:T(1024)S(1)} all-reduce(f32[2048]{0:T(1024)S(1)} %bitcast.742), channel_id=1, replica_groups=mesh['tp'=2,'dp'=8] {'tp','dp'}, use_global_device_ids=true, to_apply=%region_33.34 | all-reduce | flops 2048 | bytes 16384 | tf_op jit(solution)/shard_map/psum | solution.py:28
  722.6 117.6 %all-reduce.3.cloned.1.call-done = f32[2048,2048]{0,1:T(8,128)} async-done(((f32[2048,2048]{0,1:T(8,128)}), f32[2048,2048]{0,1:T(8,128)}) %all-reduce.3.cloned.1.call-update) | async-done | bytes 16777232 | tf_op jit(solution)/shard_map/psum | solution.py:27
  840.2 12.5 select_add_fusion
  852.6 17.6 %copy.75 = f32[2048,2048]{1,0:T(8,128)} copy(f32[2048,2048]{0,1:T(8,128)} %select_add_fusion) | data formatting | bytes 33554432 | tf_op jit(solution)/shard_map/add | solution.py:29
  870.2 12.1 fusion
  888.1 11.7 cholesky.456
  914.4 11.7 cholesky.479
  949.7 11.7 cholesky.502
  980.4 11.7 cholesky.523
  1110.4 12.1 cholesky.1020
  1143.7 11.9 cholesky.1040
  1176.7 11.9 cholesky.1060
  1209.2 12.1 cholesky.1080
  1241.3 11.9 cholesky.1100
  1272.1 11.9 cholesky.1120
  1301.9 12.1 cholesky.1140
  1389.6 12.5 select_select_fusion
  1402.1 56.4 %while.1 = (s32[]{:T(128)}, f32[2048,2048]{0,1:T(8,128)}, s32[16,2]{0,1:T(2,128)S(1)}, f32[16,128,128]{2,1,0:T(8,128)}, s32[]{:T(128)}) while((s32[]{:T(128)}, f32[2048,2048]{0,1:T(8,128)}, s32[16,2]{0,1:T(2,128)S(1)}, f32[16,128,128]{2,1,0:T(8,128)}, s32[]{:T(128)}) %tuple.163), condition=%wide.while_cond, body=%wide.while_body.sunk | while | flops 2 | bytes 393329 | solution.py:12
  1458.5 158.2 %custom-call.143 = f32[16,128,128]{1,2,0:T(8,128)S(1)} custom-call(f32[16,128,128]{2,1,0:T(8,128)} %get-tuple-element.9), custom_call_target="InvertDiagBlocksLowerTriangular" | custom-call | tf_op jit(solution)/shard_map/triangular_solve | solution.py:12
  1670.1 30.7 %fusion.214 = f32[1,8192]{1,0:T(1,128)S(1)} fusion(f32[8192,1024]{1,0:T(8,128)} %param.3, f32[2048,1]{0,1:T(1,128)S(1)} %constant_dynamic-update-slice_fusion.220, s32[]{:T(128)S(6)} %select_n.12), kind=kOutput, calls=%fused_computation.545 | convolution fusion | flops 100663296 | bytes 33591300 | tf_op jit(solution)/shard_map/dot_general | solution.py:32
  (402 shorter events, 483.8 us)
Async XLA Ops:
  7.2 833.0 %all-reduce.3.cloned.1.call-start = ((), (), s32[]{:S(2)}) async-start(), calls=%async_computation.1 | async-start | bytes 33554432 | tf_op jit(solution)/shard_map/psum | solution.py:27
  658.5 0.8 copy-start.2
  882.3 5.7 copy-start.1
  939.6 5.7 copy-start
  1670.1 30.7 %copy-start.3 = (f32[2048,1]{0,1:T(1,128)}, f32[2048,1]{0,1:T(1,128)S(1)}, u32[]{:S(2)}) copy-start(f32[2048,1]{0,1:T(1,128)S(1)} %constant_dynamic-update-slice_fusion.220) | copy-start | bytes 24580
Sparse Core Ops, SparseCore 0:
  658.6 181.4 all-reduce.2
where the time goes:
time: 1730 us; the launch traced here: 1720 us
  other arithmetic  544 us (31%)
  matrix products  461 us (27%)
  blocking collectives  436 us (25%)
  local copies, waits for them, and re-layouts  131 us (8%)
  waiting for transfers between devices  118 us (7%)
  between operations  26.2 us (2%)
    all_to_all x1, blocking collectives, local_fit(): row_panel = lax.all_to_all(design_blk, 'tp', 0, 1, tiled=True)  396 us
    another operation x62, other arithmetic, local_fit(): jnp.linalg.cholesky(gram_mat + ridge * jnp.eye(features, dtype=jnp.float32))  348 us
    dot_general x1, matrix products, local_fit(): lax.dot_general(row_panel, row_panel, CONTRACT_ROWS, precision=HIGHEST, p...  224 us
    another operation x3, other arithmetic, solve_factored(): lax.linalg.triangular_solve(chol_low, half_solve, left_side=True, lower=T...  171 us
    another operation x30, matrix products, local_fit(): jnp.linalg.cholesky(gram_mat + ridge * jnp.eye(features, dtype=jnp.float32))  124 us
    psum x1, waiting for transfers between devices, local_fit(): gram_mat = lax.psum(gram_part, ('tp', 'dp'))  118 us
    another operation x80, local copies, waits for them, and re-layouts  56.2 us
  transfers between devices with their start and end apart: 1, of which 1 were waited for; matrix products, arithmetic and copies ran while one was open for 2% of the time, Pallas kernels for 0%

commit v1 on v0

v1 whole, which is shorter than its diff:
```python
import functools

import jax
import jax.numpy as jnp
from jax import lax
from jax.experimental import pallas as pl
from jax.experimental.pallas import tpu as pltpu
from jax.sharding import PartitionSpec as P


HIGHEST = lax.Precision.HIGHEST
CONTRACT_ROWS = (((0,), (0,)), ((), ()))
SUB = 128
BLK = 2 * SUB
CHUNKS = (256, 256, 256, 128, 128)
SWAP = ((0, 1), (1, 0))
TILE = 512


def mm(a, b):
    return jnp.dot(a, b, precision=HIGHEST, preferred_element_type=jnp.float32)


def tri(i, j):
    return (i * (i - 1)) // 2 + j


def eliminate(rows, aug, put):
    sub = lax.broadcasted_iota(jnp.int32, (8, SUB), 0)
    full = lambda x: jnp.broadcast_to(x, (8, SUB))

    def octet(low, m, carry):
        pick = lambda x, c: jnp.take_along_axis(x, jnp.full((8, SUB), 8 * m + c, jnp.int32), axis=1, mode="promise_in_bounds")
        at = pl.ds(pl.multiple_of(8 * m, 8), 8)
        row, add = rows[at, :], aug[at, :]
        diag = [pick(row, c) for c in range(8)]
        spans = [slice(8 * v, 8 * v + 8) for v in range(low + 1, SUB // 8)]
        cols = [[pick(rows[span, :], c) for c in range(8)] for span in spans]
        piv_rows, aug_rows, recips, links = [], [], [], []
        pivots = jnp.ones((8, SUB), jnp.float32)
        for j in range(8):
            pivot = full(diag[j][j : j + 1, :])
            recip = 1.0 / pivot
            pivots = jnp.where(sub == j, pivot, pivots)
            mult = jnp.where(sub > j, diag[j] * recip, 0.0)
            pr, ar = full(row[j : j + 1, :]), full(add[j : j + 1, :])
            row, add = row - mult * pr, add - mult * ar
            link = {}
            for c in range(j + 1, 8):
                link[c] = full(diag[c][j : j + 1, :])
                diag[c] = diag[c] - mult * link[c]
            piv_rows.append(pr)
            aug_rows.append(ar)
            recips.append(recip)
            links.append(link)
        put(m, add * lax.rsqrt(pivots))
        for span, col in zip(spans, cols):
            r, e = rows[span, :], aug[span, :]
            for j in range(8):
                mult = col[j] * recips[j]
                r = r - mult * piv_rows[j]
                e = e - mult * aug_rows[j]
                for c in range(j + 1, 8):
                    col[c] = col[c] - mult * links[j][c]
            rows[span, :] = r
            aug[span, :] = e
        return carry

    for low in range(0, SUB // 8, 4):
        lax.fori_loop(low, low + 4, functools.partial(octet, low), 0)


def factor_kernel(first, steps, source, last, n_cc, *refs):
    ridge, gram_hbm = refs[0], refs[1]
    cc_hbm = refs[2 : 2 + n_cc]
    refs = refs[2 + n_cc :]
    if first:
        refs = refs[3:]
    low_hbm, inv_hbm, half_hbm = refs[0], refs[1], refs[2]
    refs = refs[3:]
    if last:
        x_ref, refs = refs[0], refs[1:]
    low, inv, half, diag, cross, prev, mom, panel, work, acc, up, rows, aug, sems, wsems = refs
    end = first + steps
    width = SUB * steps
    loads = []

    def load(src, dst):
        copy = pltpu.make_async_copy(src, dst, sems.at[len(loads)])
        copy.start()
        loads.append(copy)

    load(gram_hbm.at[:, pl.ds(0, end), pl.ds(0, SUB), pl.ds(SUB * first, width)], diag.at[:, pl.ds(0, end), :, pl.ds(0, width)])
    load(gram_hbm.at[:, 0, pl.ds(SUB, 8), :], mom)
    load(cc_hbm[source[first][0]].at[:, pl.ds(0, end)], cross.at[:, pl.ds(0, end), :, pl.ds(0, width)])
    for st in range(steps):
        for i in range(first + st):
            arr, col = source[i]
            load(cc_hbm[arr].at[:, first + st, :, pl.ds(col, SUB)], prev.at[st, i])
    if first:
        load(inv_hbm.at[pl.ds(0, first)], inv.at[pl.ds(0, first)])
        load(half_hbm.at[pl.ds(0, first)], half.at[pl.ds(0, first)])
        if first > 1:
            load(low_hbm.at[pl.ds(0, tri(first, 0))], low.at[pl.ds(0, tri(first, 0))])
    for copy in loads:
        copy.wait()
    lam = ridge[0, 0]

    def step(st, carry):
        k = first + st
        lanes = pl.ds(pl.multiple_of(st * SUB, SUB), SUB)

        def substitute(i, carry):
            work[0:SUB, 0:SUB] = diag[0, i, :, lanes]
            work[SUB:BLK, SUB:BLK] = diag[1, i, :, lanes]
            work[0:SUB, SUB:BLK] = cross[0, i, :, lanes] + prev[st, i, 1].T
            work[SUB:BLK, 0:SUB] = cross[1, i, :, lanes] + prev[st, i, 0].T

            def reduce(j, carry):
                work[...] -= mm(low[tri(i, 0) + j], panel[j])
                return carry

            lax.fori_loop(0, i, reduce, 0)
            panel[i] = mm(inv[i, 0], work[...])
            return carry

        lax.fori_loop(0, k, substitute, 0)
        eye = lax.broadcasted_iota(jnp.int32, (SUB, SUB), 0) == lax.broadcasted_iota(jnp.int32, (SUB, SUB), 1)
        shift = jnp.where(eye, lam, 0.0)
        off = cross[0, k, :, lanes] + cross[1, k, :, lanes].T
        work[0:SUB, 0:SUB] = diag[0, k, :, lanes] + shift
        work[SUB:BLK, SUB:BLK] = diag[1, k, :, lanes] + shift
        work[0:SUB, SUB:BLK] = off
        work[SUB:BLK, 0:SUB] = off.T

        def schur(j, carry):
            flipped = panel[j].T
            low[tri(k, 0) + j] = flipped
            work[...] -= mm(flipped, panel[j])
            return carry

        lax.fori_loop(0, k, schur, 0)

        def factor(b, carry):
            at = pl.ds(pl.multiple_of(b * SUB, SUB), SUB)
            rows[...] = work[at, at]
            aug[...] = jnp.where(eye, 1.0, 0.0).astype(jnp.float32)

            def put(m, block):
                inv[k, 0, pl.ds(pl.multiple_of(b * SUB + 8 * m, 8), 8), at] = block

            eliminate(rows, aug, put)

            @pl.when(b == 0)
            def _():
                upper = mm(inv[k, 0, 0:SUB, 0:SUB], work[0:SUB, SUB:BLK])
                flipped = upper.T
                up[...] = flipped
                work[SUB:BLK, SUB:BLK] -= mm(flipped, upper)

            return carry

        lax.fori_loop(0, 2, factor, 0)
        inv[k, 0, 0:SUB, SUB:BLK] = jnp.zeros((SUB, SUB), jnp.float32)
        inv[k, 0, SUB:BLK, 0:SUB] = -mm(inv[k, 0, SUB:BLK, SUB:BLK], mm(up[...], inv[k, 0, 0:SUB, 0:SUB]))
        inv[k, 1] = inv[k, 0].T
        at = pl.ds(pl.multiple_of(k * SUB, SUB), SUB)
        rhs = jnp.concatenate([mom[0, 0:1, at], mom[1, 0:1, at]], axis=1)
        rhs = jnp.broadcast_to(rhs, (SUB, BLK)).T[:, 0:1]

        def forward(j, rhs):
            return rhs - jnp.sum(low[tri(k, 0) + j] * half[j, 0:1, :], axis=1, keepdims=True)

        rhs = lax.fori_loop(0, k, forward, rhs)
        half[k] = jnp.broadcast_to(jnp.sum(inv[k, 1] * rhs, axis=0, keepdims=True), (8, BLK))
        return carry

    lax.fori_loop(0, steps, step, 0)
    stores = []

    def store(src, dst):
        copy = pltpu.make_async_copy(src, dst, wsems.at[len(stores)])
        copy.start()
        stores.append(copy)

    if not last:
        store(inv.at[pl.ds(first, steps)], inv_hbm.at[pl.ds(first, steps)])
        store(half.at[pl.ds(first, steps)], half_hbm.at[pl.ds(first, steps)])
        if tri(end, 0) > tri(first, 0):
            span = pl.ds(tri(first, 0), tri(end, 0) - tri(first, 0))
            store(low.at[span], low_hbm.at[span])
        for copy in stores:
            copy.wait()
        return
    acc[...] = jnp.zeros_like(acc)

    def backward(t, carry):
        k = end - 1 - t
        rhs = half[k, 0:1, :] - acc[k, 0:1, :]
        col = jnp.sum(inv[k, 1] * rhs, axis=1, keepdims=True)
        row = jnp.broadcast_to(col, (BLK, SUB)).T[0:1, :]
        at = pl.ds(pl.multiple_of(k * SUB, SUB), SUB)
        x_ref[0:1, at] = row[:, 0:SUB]
        x_ref[1:2, at] = row[:, SUB:BLK]

        def spread(j, carry):
            acc[j, 0:1, :] += jnp.sum(low[tri(k, 0) + j] * col, axis=0, keepdims=True)
            return carry

        lax.fori_loop(0, k, spread, 0)
        return carry

    lax.fori_loop(0, end, backward, 0)


def factor_call(first, steps, source, last, n_blocks, ridge, gram, ccs, state):
    n_low = tri(n_blocks, 0)
    shapes = [
        jax.ShapeDtypeStruct((n_low, BLK, BLK), jnp.float32),
        jax.ShapeDtypeStruct((n_blocks, 2, BLK, BLK), jnp.float32),
        jax.ShapeDtypeStruct((n_blocks, 8, BLK), jnp.float32),
    ]
    hbm = pl.BlockSpec(memory_space=pltpu.HBM)
    in_specs = [pl.BlockSpec(memory_space=pltpu.SMEM)] + [hbm] * (1 + len(ccs))
    args = [ridge, gram, *ccs]
    aliases = {}
    if first:
        aliases = {len(args) + n: n for n in range(3)}
        in_specs += [hbm] * 3
        args += list(state)
    out_shape, out_specs = list(shapes), [hbm] * 3
    if last:
        out_shape.append(jax.ShapeDtypeStruct((2, n_blocks * SUB), jnp.float32))
        out_specs.append(pl.BlockSpec(memory_space=pltpu.VMEM))
    wide = (2, n_blocks, SUB, BLK)
    res = pl.pallas_call(
        functools.partial(factor_kernel, first, steps, source, last, len(ccs)),
        out_shape=out_shape,
        in_specs=in_specs,
        out_specs=out_specs,
        input_output_aliases=aliases,
        scratch_shapes=[
            pltpu.VMEM((n_low, BLK, BLK), jnp.float32),
            pltpu.VMEM((n_blocks, 2, BLK, BLK), jnp.float32),
            pltpu.VMEM((n_blocks, 8, BLK), jnp.float32),
            pltpu.VMEM(wide, jnp.float32),
            pltpu.VMEM(wide, jnp.float32),
            pltpu.VMEM((2, n_blocks, 2, SUB, SUB), jnp.float32),
            pltpu.VMEM((2, 8, n_blocks * SUB), jnp.float32),
            pltpu.VMEM((n_blocks, BLK, BLK), jnp.float32),
            pltpu.VMEM((BLK, BLK), jnp.float32),
            pltpu.VMEM((n_blocks, 8, BLK), jnp.float32),
            pltpu.VMEM((SUB, SUB), jnp.float32),
            pltpu.VMEM((SUB, SUB), jnp.float32),
            pltpu.VMEM((SUB, SUB), jnp.float32),
            pltpu.SemaphoreType.DMA((32,)),
            pltpu.SemaphoreType.DMA((4,)),
        ],
        compiler_params=pltpu.CompilerParams(vmem_limit_bytes=48 * 1024 * 1024),
        cost_estimate=pl.CostEstimate(flops=int(2e10) * steps, bytes_accessed=8 << 20, transcendentals=0),
    )(*args)
    return res[:3], (res[3] if last else None)


def moment_kernel(design, target, out, acc):
    i = pl.program_id(0)

    @pl.when(i == 0)
    def _():
        acc[...] = jnp.zeros_like(acc)

    for q in range(design.shape[0] // SUB):
        col = jnp.broadcast_to(target[pl.ds(i * (design.shape[0] // SUB) + q, 1), :], (SUB, SUB)).T
        for g in range(0, design.shape[1], SUB):
            prod = design[SUB * q : SUB * q + SUB, g : g + SUB] * col
            acc[:, g : g + SUB] += jnp.sum(prod.reshape(SUB // 8, 8, SUB), axis=0)

    @pl.when(i == pl.num_programs(0) - 1)
    def _():
        out[...] = jnp.broadcast_to(jnp.sum(acc[...], axis=0, keepdims=True), out.shape)


def moment_call(design, target):
    rows, cols = design.shape
    return pl.pallas_call(
        moment_kernel,
        grid=(rows // TILE,),
        out_shape=jax.ShapeDtypeStruct((8, cols), jnp.float32),
        in_specs=[pl.BlockSpec((TILE, cols), lambda i: (i, 0)), pl.BlockSpec((rows // SUB, SUB), lambda i: (0, 0))],
        out_specs=pl.BlockSpec((8, cols), lambda i: (0, 0)),
        scratch_shapes=[pltpu.VMEM((8, cols), jnp.float32)],
        compiler_params=pltpu.CompilerParams(vmem_limit_bytes=16 << 20),
        cost_estimate=pl.CostEstimate(flops=int(1e10), bytes_accessed=4 * rows * cols, transcendentals=0),
        name="moment",
    )(design, target.reshape(rows // SUB, SUB))


def fit_kernel(design, coeff, out):
    i = pl.program_id(0)
    for q in range(design.shape[0] // SUB):
        prod = sum(design[SUB * q : SUB * q + SUB, g : g + SUB] * coeff[0:1, g : g + SUB] for g in range(0, design.shape[1], SUB))
        out[pl.ds(i * (design.shape[0] // SUB) + q, 1), :] = jnp.sum(prod.T, axis=0, keepdims=True)


def fit_call(design, coeff):
    rows, cols = design.shape
    return pl.pallas_call(
        fit_kernel,
        grid=(rows // TILE,),
        out_shape=jax.ShapeDtypeStruct((rows // SUB, SUB), jnp.float32),
        in_specs=[pl.BlockSpec((TILE, cols), lambda i: (i, 0)), pl.BlockSpec((1, cols), lambda i: (0, 0))],
        out_specs=pl.BlockSpec((rows // SUB, SUB), lambda i: (0, 0)),
        compiler_params=pltpu.CompilerParams(vmem_limit_bytes=16 << 20),
        cost_estimate=pl.CostEstimate(flops=int(1e10), bytes_accessed=4 * rows * cols, transcendentals=0),
        name="fit",
    )(design, coeff)


def after(value, *deps):
    return lax.optimization_barrier((value, *deps))[0]


def solution(mesh):
    groups = mesh.shape["dp"]

    def local_fit(design, target, ridge):
        rows, cols = design.shape
        part = rows // 2
        side = lax.axis_index("tp")

        def gram_of(lhs, rhs):
            return lax.dot_general(lhs, rhs, CONTRACT_ROWS, precision=HIGHEST, preferred_element_type=jnp.float32)

        def scatter(partial):
            return lax.psum_scatter(partial, "dp", scatter_dimension=0, tiled=False)

        def gather(mine):
            whole = lax.all_gather(mine, ("tp", "dp"), axis=0, tiled=False)
            return whole.reshape(2, groups, *mine.shape)

        starts = [sum(CHUNKS[:n]) for n in range(len(CHUNKS))]
        arrived = []
        for at, width in zip(starts, CHUNKS):
            piece = lax.dynamic_slice(design, (side * part, at), (part, width))
            arrived.append(lax.ppermute(piece, "tp", SWAP))
        kept = lax.dynamic_slice_in_dim(design, (1 - side) * part, part)

        top = gram_of(design[:, : cols // 2], design)
        end = gram_of(design[:, cols // 2 :], design[:, cols // 2 :])
        moment = moment_call(design, after(target, top, end))
        own = jnp.concatenate([top, jnp.pad(end, ((0, 0), (cols // 2, 0)))], axis=0).reshape(groups, cols // groups, cols)
        extra = jnp.pad(moment[None], ((0, groups - 1), (0, 0), (0, 0)))
        gram_rs = scatter(jnp.concatenate([own, extra], axis=1))

        def cross(n, *deps):
            return scatter(gram_of(kept, after(arrived[n], *deps)).reshape(groups, cols // groups, CHUNKS[n]))

        source = []
        for n, width in enumerate(CHUNKS):
            source += [(n, c) for c in range(0, width, SUB)]
        lam = ridge.reshape(1, 1)
        ccs, counts = [], [width // SUB for width in CHUNKS]

        def factor(n, state, *deps):
            first = sum(counts[:n])
            return factor_call(
                first, counts[n], tuple(source[: first + counts[n]]), n == len(CHUNKS) - 1, cols // SUB,
                after(lam, *deps), gram, ccs[: n + 1], state,
            )

        rs0 = cross(0, moment)
        rs1 = cross(1, gram_rs)
        gram = gather(after(gram_rs, rs0))
        ccs.append(gather(after(rs0, gram_rs)))
        ccs.append(gather(rs1))
        state, _ = factor(0, None, rs1)
        rs2 = cross(2, *state)
        ccs.append(gather(rs2))
        state, _ = factor(1, state, rs2)
        rs3 = cross(3, *state, rs2)
        ccs.append(gather(rs3))
        rs4 = cross(4, rs3)
        ccs.append(gather(rs4))
        state, _ = factor(2, state, rs3)
        state, _ = factor(3, state, rs4)
        _, coeff = factor(4, state)

        mine = lax.dynamic_slice_in_dim(coeff, side, 1)
        fit = fit_call(design, mine)
        fitted = fit + lax.ppermute(fit, "tp", SWAP)
        return coeff.reshape(2 * cols), target - fitted.reshape(rows)

    return jax.shard_map(local_fit, mesh=mesh, in_specs=(P("dp", "tp"), P("dp"), P()), out_specs=(P(), P("dp")), check_vma=False)
```

time: 1730 us -> 869 us (0.50)
  other arithmetic: 544 us -> 3.91 us
  blocking collectives: 436 us -> 0 us
  waiting for transfers between devices: 118 us -> 382 us
  matrix products: 461 us -> 240 us
  Pallas kernels: 0 us -> 164 us
  local copies, waits for them, and re-layouts: 131 us -> 45.3 us
    another operation x65 -> x0, other arithmetic: 519 us -> none  [the longest x62 348 us: local_fit(): jnp.linalg.cholesky(gram_mat + ridge * jnp.eye(features, dtype=jnp.float32))]
    all_to_all x1 -> x0, blocking collectives: 396 us -> none  [local_fit(): row_panel = lax.all_to_all(design_blk, 'tp', 0, 1, tiled=True)]
    another operation x92 -> x0, matrix products: 175 us -> none  [the longest x30 124 us: local_fit(): jnp.linalg.cholesky(gram_mat + ridge * jnp.eye(features, dtype=jnp.float32))]
    pallas_call x0 -> x7, Pallas kernels: none -> 164 us  [the longest x5 158 us: factor_call(): pl.pallas_call(functools.partial(factor_kernel, first, steps, source, las...]
    ppermute x0 -> x6, waiting for transfers between devices: none -> 152 us  [the longest x5 150 us: local_fit(): arrived.append(lax.ppermute(piece, 'tp', SWAP))]
    all_gather x0 -> x6, waiting for transfers between devices: none -> 149 us  [gather(): whole = lax.all_gather(mine, ('tp', 'dp'), axis=0, tiled=False)]
    psum x1 -> x0, waiting for transfers between devices: 118 us -> none  [local_fit(): gram_mat = lax.psum(gram_part, ('tp', 'dp'))]
    reduce_scatter x0 -> x6, waiting for transfers between devices: none -> 77.8 us  [scatter(): return lax.psum_scatter(partial, 'dp', scatter_dimension=0, tiled=False)]
  transfers between devices with their start and end apart: 1 -> 18, of which waited for: 1 -> 9; matrix products, arithmetic and copies ran while one was open for 2% -> 16% of each run, Pallas kernels for 0% -> 14%
where the time goes in v1:
time: 869 us; the launch traced here: 859 us
  waiting for transfers between devices  382 us (44%)
  matrix products  240 us (28%)
  Pallas kernels  164 us (19%)
  local copies, waits for them, and re-layouts  45.3 us (5%)
  between operations  15.3 us (2%)
  starting transfers between devices  9.11 us (1%)
    dot_general x7, matrix products, gram_of(): lax.dot_general(lhs, rhs, CONTRACT_ROWS, precision=HIGHEST, preferred_ele...  240 us
    pallas_call x5, Pallas kernels, factor_call(): pl.pallas_call(functools.partial(factor_kernel, first, steps, source, las...  158 us
    ppermute x5, waiting for transfers between devices, local_fit(): arrived.append(lax.ppermute(piece, 'tp', SWAP))  150 us
    all_gather x6, waiting for transfers between devices, gather(): whole = lax.all_gather(mine, ('tp', 'dp'), axis=0, tiled=False)  149 us
    reduce_scatter x6, waiting for transfers between devices, scatter(): return lax.psum_scatter(partial, 'dp', scatter_dimension=0, tiled=False)  77.8 us
    unnamed x25, local copies, waits for them, and re-layouts  30.6 us
  transfers between devices with their start and end apart: 18, of which 9 were waited for; matrix products, arithmetic and copies ran while one was open for 16% of the time, Pallas kernels for 14%

profile of v1, /device:TPU:0, one launch (start us, length us, event | category | flops | bytes accessed | tf_op | source)
XLA Modules:
  0.0 859.5 jit_solution(11173476532403174959)
XLA Ops:
  7.2 58.4 %fusion.2 = f32[512,1024]{1,0:T(8,128)S(1)} fusion(f32[8192,1024]{1,0:T(8,128)} %design.3), kind=kOutput, calls=%fused_computation.2 | convolution fusion | flops 51539607552 | bytes 52428800 | tf_op jit(solution)/shard_map/dot_general | solution.py:332
  65.6 30.7 %fusion = f32[512,512]{1,0:T(8,128)S(1)} fusion(f32[8192,1024]{1,0:T(8,128)} %design.3), kind=kOutput, calls=%fused_computation | convolution fusion | flops 25769803776 | bytes 17825792 | tf_op jit(solution)/shard_map/dot_general | solution.py:332
  97.0 10.5 %copy-done = f32[8192,1024]{1,0:T(8,128)S(1)} copy-done((f32[8192,1024]{1,0:T(8,128)S(1)}, f32[8192,1024]{1,0:T(8,128)}, u32[]{:S(2)}) %copy-start) | copy-done | bytes 33554456
  113.8 10.1 %constant_dynamic-slice_fusion.4 = (f32[4096,256]{1,0:T(8,128)}, f32[4096,256]{1,0:T(8,128)}, f32[4096,256]{1,0:T(8,128)}) fusion(f32[8192,1024]{1,0:T(8,128)} %design.3, s32[]{:T(128)S(6)} %select_n.14), kind=kLoop, calls=%fused_computation.29 | loop fusion | bytes 25165828 | tf_op jit(solution)/shard_map/dynamic_slice | solution.py:344
  127.3 91.7 %collective-permute-done = f32[4096,256]{1,0:T(8,128)} collective-permute-done((f32[4096,256]{1,0:T(8,128)}, f32[4096,256]{1,0:T(8,128)}, u32[]{:S(2)}, u32[]{:S(2)}) %collective-permute-start) | collective-permute-done | bytes 4194336 | tf_op jit(solution)/shard_map/ppermute | solution.py:345
  219.0 30.3 %fusion.12 = f32[1024,256]{1,0:T(8,128)} fusion(f32[4096,256]{1,0:T(8,128)} %collective-permute-done, f32[8192,1024]{1,0:T(8,128)} %design.3, s32[]{:T(128)S(6)} %select_n.6), kind=kOutput, calls=%fused_computation.12 | convolution fusion | flops 12884901888 | bytes 22020100 | tf_op jit(solution)/shard_map/dot_general | solution.py:332
  249.4 58.6 %collective-permute-done.1 = f32[4096,256]{1,0:T(8,128)} collective-permute-done((f32[4096,256]{1,0:T(8,128)}, f32[4096,256]{1,0:T(8,128)}, u32[]{:S(2)}, u32[]{:S(2)}) %collective-permute-start.1) | collective-permute-done | bytes 4194336 | tf_op jit(solution)/shard_map/ppermute | solution.py:345
  308.0 30.4 %fusion.10 = f32[1024,256]{1,0:T(8,128)} fusion(f32[4096,256]{1,0:T(8,128)} %collective-permute-done.1, f32[8192,1024]{1,0:T(8,128)} %design.3, s32[]{:T(128)S(6)} %select_n.6), kind=kOutput, calls=%fused_computation.10 | convolution fusion | flops 12884901888 | bytes 22020100 | tf_op jit(solution)/shard_map/dot_general | solution.py:332
  341.4 4.6 constant_dynamic-slice_fusion.2
  348.6 21.5 %reduce-scatter.11.cloned.1.call-done = f32[1,128,256]{2,1,0:T(8,128)} async-done(((f32[8,128,256]{2,1,0:T(8,128)}), f32[1,128,256]{2,1,0:T(8,128)}) %reduce-scatter.11.cloned.1.call-update) | async-done | bytes 131088 | tf_op jit(solution)/shard_map/reduce_scatter | solution.py:335
  370.2 37.5 %all-gather.19.cloned.1.call-done = f32[2048,256]{1,0:T(8,128)} async-done(((f32[128,256]{1,0:T(8,128)}), f32[2048,256]{1,0:T(8,128)}) %all-gather.19.cloned.1.call-update) | async-done | bytes 2097168 | tf_op jit(solution)/shard_map/all_gather | solution.py:338
  407.7 81.0 %all-gather.17.cloned.1.call-done = f32[2176,1024]{1,0:T(8,128)} async-done(((f32[136,1024]{1,0:T(8,128)}), f32[2176,1024]{1,0:T(8,128)}) %all-gather.17.cloned.1.call-update) | async-done | bytes 8912912 | tf_op jit(solution)/shard_map/all_gather | solution.py:338
  490.3 24.5 %shard_map.50 = (f32[28,256,256]{2,1,0:T(8,128)}, f32[8,2,256,256]{3,2,1,0:T(8,128)}, f32[8,8,256]{2,1,0:T(8,128)S(1)}) custom-call(f32[1,1]{1,0:T(1,128)} %bitcast.32.refs_0_, f32[2,8,136,1024]{3,2,1,0:T(8,128)} %bitcast.61, f32[2,8,128,256]{3,2,1,0:T(8,128)S(1)} %bitcast.40), custom_call_target="tpu_custom_call" | custom-call | flops 40000000000 | bytes 8388608 | tf_op jit(solution)/shard_map/pallas_call | solution.py:236
  514.8 30.4 %fusion.8 = f32[1024,256]{1,0:T(8,128)} fusion(f32[4096,256]{1,0:T(8,128)} %collective-permute-done.2, f32[8192,1024]{1,0:T(8,128)} %design.3, s32[]{:T(128)S(6)} %select_n.6), kind=kOutput, calls=%fused_computation.8 | convolution fusion | flops 12884901888 | bytes 22020100 | tf_op jit(solution)/shard_map/dot_general | solution.py:332
  546.9 31.3 %shard_map.51 = (f32[28,256,256]{2,1,0:T(8,128)}, f32[8,2,256,256]{3,2,1,0:T(8,128)}, f32[8,8,256]{2,1,0:T(8,128)S(1)}) custom-call(f32[1,1]{1,0:T(1,128)} %bitcast.35.refs_0_, f32[2,8,136,1024]{3,2,1,0:T(8,128)} %bitcast.62, f32[2,8,128,256]{3,2,1,0:T(8,128)S(1)} %bitcast.41, ...), custom_call_target="tpu_custom_call", output_to_operand_aliasing={{0}: (4, {}), {1}: (5, {}), {2}: (6, {})} | custom-call | flops 40000000000 | bytes 8388608 | tf_op jit(solution)/shard_map/pallas_call | solution.py:236
  578.2 29.8 %fusion.6 = f32[1024,128]{1,0:T(8,128)} fusion(f32[4096,128]{1,0:T(8,128)} %collective-permute-done.3, f32[8192,1024]{1,0:T(8,128)} %design.3, s32[]{:T(128)S(6)} %select_n.6), kind=kOutput, calls=%fused_computation.6 | convolution fusion | flops 6442450944 | bytes 19398660 | tf_op jit(solution)/shard_map/dot_general | solution.py:332
  608.1 28.9 %reduce-scatter.15.cloned.1.call-done = f32[1,128,128]{2,1,0:T(8,128)} async-done(((f32[8,128,128]{2,1,0:T(8,128)}), f32[1,128,128]{2,1,0:T(8,128)}) %reduce-scatter.15.cloned.1.call-update) | async-done | bytes 65552 | tf_op jit(solution)/shard_map/reduce_scatter | solution.py:335
  637.0 30.0 %fusion.4 = f32[1024,128]{1,0:T(8,128)} fusion(f32[4096,128]{1,0:T(8,128)} %collective-permute-done.4, f32[8192,1024]{1,0:T(8,128)} %design.3, s32[]{:T(128)S(6)} %select_n.6), kind=kOutput, calls=%fused_computation.4 | convolution fusion | flops 6442450944 | bytes 19398660 | tf_op jit(solution)/shard_map/dot_general | solution.py:332
  668.4 27.3 %reduce-scatter.17.cloned.1.call-done = f32[1,128,128]{2,1,0:T(8,128)} async-done(((f32[8,128,128]{2,1,0:T(8,128)}), f32[1,128,128]{2,1,0:T(8,128)}) %reduce-scatter.17.cloned.1.call-update) | async-done | bytes 65552 | tf_op jit(solution)/shard_map/reduce_scatter | solution.py:335
  695.7 30.7 %all-gather.11.cloned.1.call-done = f32[16,128,256]{2,1,0:T(8,128)} async-done(((f32[1,128,256]{2,1,0:T(8,128)}), f32[16,128,256]{2,1,0:T(8,128)}) %all-gather.11.cloned.1.call-update) | async-done | bytes 2097168 | tf_op jit(solution)/shard_map/all_gather | solution.py:338
  728.0 41.5 %shard_map.52 = (f32[28,256,256]{2,1,0:T(8,128)}, f32[8,2,256,256]{3,2,1,0:T(8,128)}, f32[8,8,256]{2,1,0:T(8,128)S(1)}) custom-call(f32[1,1]{1,0:T(1,128)} %bitcast.36.refs_0_, f32[2,8,136,1024]{3,2,1,0:T(8,128)} %bitcast.63, f32[2,8,128,256]{3,2,1,0:T(8,128)S(1)} %bitcast.42, ...), custom_call_target="tpu_custom_call", output_to_operand_aliasing={{0}: (5, {}), {1}: (6, {}), {2}: (7, {})} | custom-call | flops 40000000000 | bytes 8388608 | tf_op jit(solution)/shard_map/pallas_call | solution.py:236
  772.4 27.3 %shard_map.53 = (f32[28,256,256]{2,1,0:T(8,128)}, f32[8,2,256,256]{3,2,1,0:T(8,128)}, f32[8,8,256]{2,1,0:T(8,128)S(1)}) custom-call(f32[1,1]{1,0:T(1,128)} %bitcast.33.refs_0_, f32[2,8,136,1024]{3,2,1,0:T(8,128)} %bitcast.64, f32[2,8,128,256]{3,2,1,0:T(8,128)S(1)} %bitcast.43, ...), custom_call_target="tpu_custom_call", output_to_operand_aliasing={{0}: (6, {}), {1}: (7, {}), {2}: (8, {})} | custom-call | flops 20000000000 | bytes 8388608 | tf_op jit(solution)/shard_map/pallas_call | solution.py:236
  801.0 32.9 %shard_map.54 = (f32[28,256,256]{2,1,0:T(8,128)}, f32[8,2,256,256]{3,2,1,0:T(8,128)}, f32[8,8,256]{2,1,0:T(8,128)S(1)}, f32[2,1024]{1,0:T(2,128)S(1)}) custom-call(f32[1,1]{1,0:T(1,128)} %bitcast.34.refs_0_, f32[2,8,136,1024]{3,2,1,0:T(8,128)} %bitcast.65, ...), custom_call_target="tpu_custom_call", output_to_operand_aliasing={{0}: (7, {}), {1}: (8, {}), {2}: (9, {})} | custom-call | flops 20000000000 | bytes 8388608 | tf_op jit(solution)/shard_map/pallas_call | solution.py:236
  833.9 10.5 %copy-done.1 = f32[8192,1024]{1,0:T(8,128)S(1)} copy-done((f32[8192,1024]{1,0:T(8,128)S(1)}, f32[8192,1024]{1,0:T(8,128)}, u32[]{:S(2)}) %copy-start.1) | copy-done | bytes 33554456
  (69 shorter events, 33.7 us)
Async XLA Ops:
  7.2 300.8 %reduce-scatter.7.cloned.1.call-start = ((), (), s32[]{:S(2)}) async-start(), calls=%async_computation.6 | async-start | bytes 5013504 | tf_op jit(solution)/shard_map/reduce_scatter | solution.py:335
  97.0 10.5 %copy-start = (f32[8192,1024]{1,0:T(8,128)S(1)}, f32[8192,1024]{1,0:T(8,128)}, u32[]{:S(2)}) copy-start(f32[8192,1024]{1,0:T(8,128)} %design.3) | copy-start | bytes 100663296
  113.8 224.7 %reduce-scatter.9.cloned.1.call-start = ((), (), s32[]{:S(2)}) async-start(), calls=%async_computation.7 | async-start | bytes 1179648 | tf_op jit(solution)/shard_map/reduce_scatter | solution.py:335
  124.0 95.0 %collective-permute-start = (f32[4096,256]{1,0:T(8,128)}, f32[4096,256]{1,0:T(8,128)}, u32[]{:S(2)}, u32[]{:S(2)}) collective-permute-start(f32[4096,256]{1,0:T(8,128)} %get-tuple-element.52), channel_id=1, source_target_pairs={{0,8},{8,0},{1,9},{9,1},{2,10},{10,2},{3,11},{11,3},{4,12},{12,4},... | collective-permute-start | bytes 12582920 | tf_op jit(solution)/shard_map/ppermute | solution.py:345
  127.2 180.7 %collective-permute-start.1 = (f32[4096,256]{1,0:T(8,128)}, f32[4096,256]{1,0:T(8,128)}, u32[]{:S(2)}, u32[]{:S(2)}) collective-permute-start(f32[4096,256]{1,0:T(8,128)} %get-tuple-element.51), channel_id=1, source_target_pairs={{0,8},{8,0},{1,9},{9,1},{2,10},{10,2},{3,11},{11,3},{4,12},{12,4},... | collective-permute-start | bytes 12582920 | tf_op jit(solution)/shard_map/ppermute | solution.py:345
  249.3 120.8 %reduce-scatter.11.cloned.1.call-start = ((), (), s32[]{:S(2)}) async-start(), calls=%async_computation.8 | async-start | bytes 1179648 | tf_op jit(solution)/shard_map/reduce_scatter | solution.py:335
  338.4 69.3 %all-gather.19.cloned.1.call-start = ((), (), s32[]{:S(2)}) async-start(), calls=%async_computation.17 | async-start | bytes 2228224 | tf_op jit(solution)/shard_map/all_gather | solution.py:338
  339.0 149.8 %all-gather.17.cloned.1.call-start = ((), (), s32[]{:S(2)}) async-start(), calls=%async_computation.16 | async-start | bytes 9469952 | tf_op jit(solution)/shard_map/all_gather | solution.py:338
  339.5 205.7 %all-gather.9.cloned.1.call-start = ((), (), s32[]{:S(2)}) async-start(), calls=%async_computation.9 | async-start | bytes 2228224 | tf_op jit(solution)/shard_map/all_gather | solution.py:338
  339.6 175.2 %collective-permute-start.2 = (f32[4096,256]{1,0:T(8,128)}, f32[4096,256]{1,0:T(8,128)}, u32[]{:S(2)}, u32[]{:S(2)}) collective-permute-start(f32[4096,256]{1,0:T(8,128)} %get-tuple-element.50), channel_id=1, source_target_pairs={{0,8},{8,0},{1,9},{9,1},{2,10},{10,2},{3,11},{11,3},{4,12},{12,4},... | collective-permute-start | bytes 12582920 | tf_op jit(solution)/shard_map/ppermute | solution.py:345
  346.0 232.2 %collective-permute-start.3 = (f32[4096,128]{1,0:T(8,128)}, f32[4096,128]{1,0:T(8,128)}, u32[]{:S(2)}, u32[]{:S(2)}) collective-permute-start(f32[4096,128]{1,0:T(8,128)} %get-tuple-element.49), channel_id=1, source_target_pairs={{0,8},{8,0},{1,9},{9,1},{2,10},{10,2},{3,11},{11,3},{4,12},{12,4},... | collective-permute-start | bytes 6291464 | tf_op jit(solution)/shard_map/ppermute | solution.py:345
  346.2 261.9 %collective-permute-start.4 = (f32[4096,128]{1,0:T(8,128)}, f32[4096,128]{1,0:T(8,128)}, u32[]{:S(2)}, u32[]{:S(2)}) collective-permute-start(f32[4096,128]{1,0:T(8,128)} %get-tuple-element.48), channel_id=1, source_target_pairs={{0,8},{8,0},{1,9},{9,1},{2,10},{10,2},{3,11},{11,3},{4,12},{12,4},... | collective-permute-start | bytes 6291464 | tf_op jit(solution)/shard_map/ppermute | solution.py:345
  370.2 208.0 %reduce-scatter.13.cloned.1.call-start = ((), (), s32[]{:S(2)}) async-start(), calls=%async_computation.10 | async-start | bytes 1179648 | tf_op jit(solution)/shard_map/reduce_scatter | solution.py:335
  514.8 30.5 %copy-start.5 = (f32[2048,256]{1,0:T(8,128)S(1)}, f32[2048,256]{1,0:T(8,128)}, u32[]{:S(2)}) copy-start(f32[2048,256]{1,0:T(8,128)} %all-gather.19.cloned.1.call-done) | copy-start | bytes 6291460
  545.2 91.8 %reduce-scatter.15.cloned.1.call-start = ((), (), s32[]{:S(2)}) async-start(), calls=%async_computation.12 | async-start | bytes 589824 | tf_op jit(solution)/shard_map/reduce_scatter | solution.py:335
  545.3 1.6 copy-start.6
  608.0 87.7 %reduce-scatter.17.cloned.1.call-start = ((), (), s32[]{:S(2)}) async-start(), calls=%async_computation.14 | async-start | bytes 589824 | tf_op jit(solution)/shard_map/reduce_scatter | solution.py:335
  667.0 59.4 %all-gather.11.cloned.1.call-start = ((), (), s32[]{:S(2)}) async-start(), calls=%async_computation.11 | async-start | bytes 2228224 | tf_op jit(solution)/shard_map/all_gather | solution.py:338
  667.6 101.9 %all-gather.13.cloned.1.call-start = ((), (), s32[]{:S(2)}) async-start(), calls=%async_computation.13 | async-start | bytes 1114112 | tf_op jit(solution)/shard_map/all_gather | solution.py:338
  668.3 131.4 %all-gather.15.cloned.1.call-start = ((), (), s32[]{:S(2)}) async-start(), calls=%async_computation.15 | async-start | bytes 1114112 | tf_op jit(solution)/shard_map/all_gather | solution.py:338
  772.4 27.4 %copy-start.10 = (f32[16,128,128]{2,1,0:T(8,128)S(1)}, f32[16,128,128]{2,1,0:T(8,128)}, u32[]{:S(2)}) copy-start(f32[16,128,128]{2,1,0:T(8,128)} %all-gather.13.cloned.1.call-done) | copy-start | bytes 3145732
  833.9 10.5 %copy-start.1 = (f32[8192,1024]{1,0:T(8,128)S(1)}, f32[8192,1024]{1,0:T(8,128)}, u32[]{:S(2)}) copy-start(f32[8192,1024]{1,0:T(8,128)} %design.3) | copy-start | bytes 100663296
  844.5 7.3 copy-start.3
  847.8 4.0 collective-permute-start.5
  (6 other events, 8.0 us)
Sparse Core Ops, SparseCore 0:
  113.9 49.7 reduce-scatter.6
  249.5 31.9 reduce-scatter.8
  338.5 31.6 reduce-scatter.10
  372.3 35.3 all-gather.18
  409.8 78.8 all-gather.16
  490.8 35.6 all-gather.8
  545.3 30.8 reduce-scatter.12
  608.2 28.8 reduce-scatter.14
  667.1 28.5 reduce-scatter.16
  697.8 28.5 all-gather.10
  728.7 25.7 all-gather.12
  756.6 25.8 all-gather.14

commit v2 on v1

--- a/solution.py
+++ b/solution.py
@@ -15,6 +15,7 @@
 CHUNKS = (256, 256, 256, 128, 128)
 SWAP = ((0, 1), (1, 0))
 TILE = 512
+PACK = 32
 
 
 def mm(a, b):
@@ -71,9 +72,9 @@
 
 
 def factor_kernel(first, steps, source, last, n_cc, *refs):
-    ridge, gram_hbm = refs[0], refs[1]
-    cc_hbm = refs[2 : 2 + n_cc]
-    refs = refs[2 + n_cc :]
+    ridge, top_hbm, rest_hbm = refs[:3]
+    cc_hbm = refs[3 : 3 + n_cc]
+    refs = refs[3 + n_cc :]
     if first:
         refs = refs[3:]
     low_hbm, inv_hbm, half_hbm = refs[0], refs[1], refs[2]
@@ -90,13 +91,32 @@
         copy.start()
         loads.append(copy)
 
-    load(gram_hbm.at[:, pl.ds(0, end), pl.ds(0, SUB), pl.ds(SUB * first, width)], diag.at[:, pl.ds(0, end), :, pl.ds(0, width)])
-    load(gram_hbm.at[:, 0, pl.ds(SUB, 8), :], mom)
-    load(cc_hbm[source[first][0]].at[:, pl.ds(0, end)], cross.at[:, pl.ds(0, end), :, pl.ds(0, width)])
+    top = top_hbm.shape[1] // SUB
+    share = 2 * PACK
+    for i in range(end):
+        if i < top:
+            load(top_hbm.at[:, pl.ds(SUB * i, SUB), pl.ds(SUB * first, width)], diag.at[:, i, :, pl.ds(0, width)])
+            continue
+        begin = max(first, i)
+        span = SUB * (end - begin)
+        for at in range(0, SUB, PACK):
+            row = SUB * (i - top) + at
+            lane = SUB * top * (row % share // PACK) + SUB * (begin - top)
+            load(rest_hbm.at[:, row // share, pl.ds(0, PACK), pl.ds(lane, span)], diag.at[:, i, pl.ds(at, PACK), pl.ds(SUB * (begin - first), span)])
+    load(rest_hbm.at[:, 0, pl.ds(PACK, 8), :], mom)
+
+    def load_cross(c, lanes, dst):
+        arr, row = source[c]
+        if arr:
+            load(cc_hbm[arr - 1].at[:, pl.ds(row, SUB), lanes], dst)
+            return
+        for q in range(SUB // PACK):
+            load(rest_hbm.at[:, row // PACK + q, pl.ds(PACK + 8, PACK), lanes], dst.at[:, pl.ds(PACK * q, PACK), :])
+
     for st in range(steps):
+        load_cross(first + st, pl.ds(0, SUB * (first + st + 1)), cross.at[st, :, :, pl.ds(0, SUB * (first + st + 1))])
         for i in range(first + st):
-            arr, col = source[i]
-            load(cc_hbm[arr].at[:, first + st, :, pl.ds(col, SUB)], prev.at[st, i])
+            load_cross(i, pl.ds(SUB * (first + st), SUB), prev.at[st, i])
     if first:
         load(inv_hbm.at[pl.ds(0, first)], inv.at[pl.ds(0, first)])
         load(half_hbm.at[pl.ds(0, first)], half.at[pl.ds(0, first)])
@@ -113,8 +133,9 @@
         def substitute(i, carry):
             work[0:SUB, 0:SUB] = diag[0, i, :, lanes]
             work[SUB:BLK, SUB:BLK] = diag[1, i, :, lanes]
-            work[0:SUB, SUB:BLK] = cross[0, i, :, lanes] + prev[st, i, 1].T
-            work[SUB:BLK, 0:SUB] = cross[1, i, :, lanes] + prev[st, i, 0].T
+            at = pl.ds(pl.multiple_of(i * SUB, SUB), SUB)
+            work[0:SUB, SUB:BLK] = cross[st, 0, :, at].T + prev[st, i, 1]
+            work[SUB:BLK, 0:SUB] = cross[st, 1, :, at].T + prev[st, i, 0]
 
             def reduce(j, carry):
                 work[...] -= mm(low[tri(i, 0) + j], panel[j])
@@ -127,7 +148,8 @@
         lax.fori_loop(0, k, substitute, 0)
         eye = lax.broadcasted_iota(jnp.int32, (SUB, SUB), 0) == lax.broadcasted_iota(jnp.int32, (SUB, SUB), 1)
         shift = jnp.where(eye, lam, 0.0)
-        off = cross[0, k, :, lanes] + cross[1, k, :, lanes].T
+        at = pl.ds(pl.multiple_of(k * SUB, SUB), SUB)
+        off = cross[st, 0, :, at].T + cross[st, 1, :, at]
         work[0:SUB, 0:SUB] = diag[0, k, :, lanes] + shift
         work[SUB:BLK, SUB:BLK] = diag[1, k, :, lanes] + shift
         work[0:SUB, SUB:BLK] = off
@@ -213,7 +235,7 @@
     lax.fori_loop(0, end, backward, 0)
 
 
-def factor_call(first, steps, source, last, n_blocks, ridge, gram, ccs, state):
+def factor_call(first, steps, source, last, n_blocks, ridge, top, rest, ccs, state):
     n_low = tri(n_blocks, 0)
     shapes = [
         jax.ShapeDtypeStruct((n_low, BLK, BLK), jnp.float32),
@@ -221,8 +243,8 @@
         jax.ShapeDtypeStruct((n_blocks, 8, BLK), jnp.float32),
     ]
     hbm = pl.BlockSpec(memory_space=pltpu.HBM)
-    in_specs = [pl.BlockSpec(memory_space=pltpu.SMEM)] + [hbm] * (1 + len(ccs))
-    args = [ridge, gram, *ccs]
+    in_specs = [pl.BlockSpec(memory_space=pltpu.SMEM)] + [hbm] * (2 + len(ccs))
+    args = [ridge, top, rest, *ccs]
     aliases = {}
     if first:
         aliases = {len(args) + n: n for n in range(3)}
@@ -232,7 +254,6 @@
     if last:
         out_shape.append(jax.ShapeDtypeStruct((2, n_blocks * SUB), jnp.float32))
         out_specs.append(pl.BlockSpec(memory_space=pltpu.VMEM))
-    wide = (2, n_blocks, SUB, BLK)
     res = pl.pallas_call(
         functools.partial(factor_kernel, first, steps, source, last, len(ccs)),
         out_shape=out_shape,
@@ -243,8 +264,8 @@
             pltpu.VMEM((n_low, BLK, BLK), jnp.float32),
             pltpu.VMEM((n_blocks, 2, BLK, BLK), jnp.float32),
             pltpu.VMEM((n_blocks, 8, BLK), jnp.float32),
-            pltpu.VMEM(wide, jnp.float32),
-            pltpu.VMEM(wide, jnp.float32),
+            pltpu.VMEM((2, n_blocks, SUB, BLK), jnp.float32),
+            pltpu.VMEM((2, 2, SUB, n_blocks * SUB), jnp.float32),
             pltpu.VMEM((2, n_blocks, 2, SUB, SUB), jnp.float32),
             pltpu.VMEM((2, 8, n_blocks * SUB), jnp.float32),
             pltpu.VMEM((n_blocks, BLK, BLK), jnp.float32),
@@ -253,7 +274,7 @@
             pltpu.VMEM((SUB, SUB), jnp.float32),
             pltpu.VMEM((SUB, SUB), jnp.float32),
             pltpu.VMEM((SUB, SUB), jnp.float32),
-            pltpu.SemaphoreType.DMA((32,)),
+            pltpu.SemaphoreType.DMA((80,)),
             pltpu.SemaphoreType.DMA((4,)),
         ],
         compiler_params=pltpu.CompilerParams(vmem_limit_bytes=48 * 1024 * 1024),
@@ -289,7 +310,7 @@
         in_specs=[pl.BlockSpec((TILE, cols), lambda i: (i, 0)), pl.BlockSpec((rows // SUB, SUB), lambda i: (0, 0))],
         out_specs=pl.BlockSpec((8, cols), lambda i: (0, 0)),
         scratch_shapes=[pltpu.VMEM((8, cols), jnp.float32)],
-        compiler_params=pltpu.CompilerParams(vmem_limit_bytes=16 << 20),
+        compiler_params=pltpu.CompilerParams(vmem_limit_bytes=40 << 20),
         cost_estimate=pl.CostEstimate(flops=int(1e10), bytes_accessed=4 * rows * cols, transcendentals=0),
         name="moment",
     )(design, target.reshape(rows // SUB, SUB))
@@ -310,10 +331,35 @@
         out_shape=jax.ShapeDtypeStruct((rows // SUB, SUB), jnp.float32),
         in_specs=[pl.BlockSpec((TILE, cols), lambda i: (i, 0)), pl.BlockSpec((1, cols), lambda i: (0, 0))],
         out_specs=pl.BlockSpec((rows // SUB, SUB), lambda i: (0, 0)),
-        compiler_params=pltpu.CompilerParams(vmem_limit_bytes=16 << 20),
+        compiler_params=pltpu.CompilerParams(vmem_limit_bytes=40 << 20),
         cost_estimate=pl.CostEstimate(flops=int(1e10), bytes_accessed=4 * rows * cols, transcendentals=0),
         name="fit",
     )(design, coeff)
+
+
+def cross_kernel(base, got, kept, out):
+    @pl.when(pl.program_id(0) == 0)
+    def _():
+        out[...] = jnp.zeros_like(out)
+
+    out[...] += lax.dot_general(got[...], kept[...], CONTRACT_ROWS, precision=HIGHEST, preferred_element_type=jnp.float32)
+
+
+def cross_call(base, got, design):
+    rows, width = got.shape
+    cols = design.shape[1]
+    return pl.pallas_call(
+        cross_kernel,
+        grid_spec=pltpu.PrefetchScalarGridSpec(
+            num_scalar_prefetch=1,
+            grid=(rows // TILE,),
+            in_specs=[pl.BlockSpec((TILE, width), lambda i, b: (i, 0)), pl.BlockSpec((TILE, cols), lambda i, b: (i + b[0], 0))],
+            out_specs=pl.BlockSpec((width, cols), lambda i, b: (0, 0)),
+        ),
+        out_shape=jax.ShapeDtypeStruct((width, cols), jnp.float32),
+        compiler_params=pltpu.CompilerParams(vmem_limit_bytes=40 << 20),
+        cost_estimate=pl.CostEstimate(flops=2 * rows * width * cols, bytes_accessed=4 * rows * (cols + width), transcendentals=0),
+    )(base, got, design)
 
 
 def after(value, *deps):
@@ -332,28 +378,32 @@
             return lax.dot_general(lhs, rhs, CONTRACT_ROWS, precision=HIGHEST, preferred_element_type=jnp.float32)
 
         def scatter(partial):
-            return lax.psum_scatter(partial, "dp", scatter_dimension=0, tiled=False)
+            return lax.psum_scatter(partial, "dp", scatter_dimension=0, tiled=True)
 
         def gather(mine):
-            whole = lax.all_gather(mine, ("tp", "dp"), axis=0, tiled=False)
-            return whole.reshape(2, groups, *mine.shape)
+            return lax.all_gather(mine, ("tp", "dp"), axis=0, tiled=True).reshape(2, -1, cols)
 
         starts = [sum(CHUNKS[:n]) for n in range(len(CHUNKS))]
-        arrived = []
+        arrived, offset = [], side * part
         for at, width in zip(starts, CHUNKS):
-            piece = lax.dynamic_slice(design, (side * part, at), (part, width))
+            piece = lax.dynamic_slice(design, (offset, at), (part, width))
+            offset = after(offset, piece)
             arrived.append(lax.ppermute(piece, "tp", SWAP))
-        kept = lax.dynamic_slice_in_dim(design, (1 - side) * part, part)
+        base = ((1 - side) * (part // TILE)).astype(jnp.int32).reshape(1)
 
         top = gram_of(design[:, : cols // 2], design)
-        end = gram_of(design[:, cols // 2 :], design[:, cols // 2 :])
-        moment = moment_call(design, after(target, top, end))
-        own = jnp.concatenate([top, jnp.pad(end, ((0, 0), (cols // 2, 0)))], axis=0).reshape(groups, cols // groups, cols)
-        extra = jnp.pad(moment[None], ((0, groups - 1), (0, 0), (0, 0)))
-        gram_rs = scatter(jnp.concatenate([own, extra], axis=1))
+        top_rs = scatter(top)
+        rest = gram_of(after(design, top)[:, cols // 2 :], design[:, cols // 2 :])
+        moment = moment_call(design, after(target, rest, top_rs))
+        top = gather(top_rs)
+        rest = rest.reshape(groups, 2, PACK, cols // 2).swapaxes(1, 2).reshape(groups, PACK, cols)
+        moment = jnp.pad(moment[None], ((0, groups - 1), (0, 0), (0, 0)))
 
         def cross(n, *deps):
-            return scatter(gram_of(kept, after(arrived[n], *deps)).reshape(groups, cols // groups, CHUNKS[n]))
+            return cross_call(after(base, *deps), arrived[n], design)
+
+        mixed = cross(0, moment).reshape(groups, CHUNKS[0] // groups, cols)
+        rest_rs = scatter(jnp.concatenate([rest, moment, mixed], axis=1).reshape(-1, cols))
 
         source = []
         for n, width in enumerate(CHUNKS):
@@ -365,25 +415,23 @@
             first = sum(counts[:n])
             return factor_call(
                 first, counts[n], tuple(source[: first + counts[n]]), n == len(CHUNKS) - 1, cols // SUB,
-                after(lam, *deps), gram, ccs[: n + 1], state,
+                after(lam, *deps), top, rest, ccs[:n], state,
             )
 
-        rs0 = cross(0, moment)
-        rs1 = cross(1, gram_rs)
-        gram = gather(after(gram_rs, rs0))
-        ccs.append(gather(after(rs0, gram_rs)))
+        rs1 = scatter(cross(1, rest_rs))
+        rest = gather(rest_rs).reshape(2, groups, -1, cols)
+        state, _ = factor(0, None)
+        rs2 = scatter(cross(2, *state, rs1))
         ccs.append(gather(rs1))
-        state, _ = factor(0, None, rs1)
-        rs2 = cross(2, *state)
+        state, _ = factor(1, state)
+        rs3 = scatter(cross(3, *state, rs2))
         ccs.append(gather(rs2))
-        state, _ = factor(1, state, rs2)
-        rs3 = cross(3, *state, rs2)
+        state, _ = factor(2, state)
+        rs4 = scatter(cross(4, *state, rs3))
         ccs.append(gather(rs3))
-        rs4 = cross(4, rs3)
+        state, _ = factor(3, state)
         ccs.append(gather(rs4))
-        state, _ = factor(2, state, rs3)
-        state, _ = factor(3, state, rs4)
-        _, coeff = factor(4, state)
+        _, coeff = factor(4, state, rs4)
 
         mine = lax.dynamic_slice_in_dim(coeff, side, 1)
         fit = fit_call(design, mine)

time: 869 us -> 751 us (0.86)
  matrix products: 240 us -> 90.4 us
  Pallas kernels: 164 us -> 273 us
  waiting for transfers between devices: 382 us -> 317 us
  local copies, waits for them, and re-layouts: 45.3 us -> 32.8 us
    dot_general x7 -> x2, matrix products: 240 us -> 90.4 us  [gram_of(): lax.dot_general(lhs, rhs, CONTRACT_ROWS, precision=HIGHEST, preferred_ele...]
    all_gather x6, waiting for transfers between devices: 149 us -> 61 us  [gather(): lax.all_gather(mine, ('tp', 'dp'), axis=0, tiled=True).reshape(2, -1, cols)]
    pallas_call x0 -> x5, Pallas kernels: none -> 80.7 us  [cross_call(): pl.pallas_call(cross_kernel, grid_spec=pltpu.PrefetchScalarGridSpec(num_s...]
    reduce_scatter x6, waiting for transfers between devices: 77.8 us -> 97.8 us  [scatter(): return lax.psum_scatter(partial, 'dp', scatter_dimension=0, tiled=True)]
    unnamed x25, local copies, waits for them, and re-layouts: 30.6 us -> 12.9 us
    pallas_call x1, Pallas kernels: 3.35 us -> 16.1 us  [fit_call(): pl.pallas_call(fit_kernel, grid=(rows // TILE,), out_shape=jax.ShapeDtype...]
    pallas_call x1, Pallas kernels: 3.5 us -> 16.1 us  [moment_call(): pl.pallas_call(moment_kernel, grid=(rows // TILE,), out_shape=jax.ShapeDt...]
    dynamic_slice x2 -> x5, local copies, waits for them, and re-layouts: 14.7 us -> 19.8 us  [local_fit(): piece = lax.dynamic_slice(design, (offset, at), (part, width))]
  transfers between devices with their start and end apart: 18 -> 18, of which waited for: 9 -> 10; matrix products, arithmetic and copies ran while one was open for 16% -> 14% of each run, Pallas kernels for 14% -> 24%
where the time goes in v2:
time: 751 us; the launch traced here: 741 us
  waiting for transfers between devices  317 us (42%)
  Pallas kernels  273 us (36%)
  matrix products  90.4 us (12%)
  local copies, waits for them, and re-layouts  32.8 us (4%)
  between operations  15.5 us (2%)
  starting transfers between devices  9.96 us (1%)
    pallas_call x5, Pallas kernels, factor_call(): pl.pallas_call(functools.partial(factor_kernel, first, steps, source, las...  160 us
    ppermute x5, waiting for transfers between devices, local_fit(): arrived.append(lax.ppermute(piece, 'tp', SWAP))  154 us
    reduce_scatter x6, waiting for transfers between devices, scatter(): return lax.psum_scatter(partial, 'dp', scatter_dimension=0, tiled=True)  97.8 us
    dot_general x2, matrix products, gram_of(): lax.dot_general(lhs, rhs, CONTRACT_ROWS, precision=HIGHEST, preferred_ele...  90.4 us
    pallas_call x5, Pallas kernels, cross_call(): pl.pallas_call(cross_kernel, grid_spec=pltpu.PrefetchScalarGridSpec(num_s...  80.7 us
    all_gather x6, waiting for transfers between devices, gather(): lax.all_gather(mine, ('tp', 'dp'), axis=0, tiled=True).reshape(2, -1, cols)  61 us
    dynamic_slice x5, local copies, waits for them, and re-layouts, local_fit(): piece = lax.dynamic_slice(design, (offset, at), (part, width))  19.8 us
    pallas_call x1, Pallas kernels, moment_call(): pl.pallas_call(moment_kernel, grid=(rows // TILE,), out_shape=jax.ShapeDt...  16.1 us
  transfers between devices with their start and end apart: 18, of which 10 were waited for; matrix products, arithmetic and copies ran while one was open for 14% of the time, Pallas kernels for 24%

profile of v2, /device:TPU:0, one launch (start us, length us, event | category | flops | bytes accessed | tf_op | source)
XLA Modules:
  0.0 740.5 jit_solution(7282814248434448067)
XLA Ops:
  14.9 59.7 %fusion.3 = f32[512,1024]{1,0:T(8,128)} fusion(f32[8192,1024]{1,0:T(8,128)} %design.3), kind=kOutput, calls=%fused_computation.3 | convolution fusion | flops 51539607552 | bytes 52428800 | tf_op jit(solution)/shard_map/dot_general | solution.py:378
  74.7 30.7 %fusion = f32[512,512]{1,0:T(8,128)S(1)} fusion(f32[8192,1024]{1,0:T(8,128)} %design.3), kind=kOutput, calls=%fused_computation | convolution fusion | flops 25769803776 | bytes 34603008 | tf_op jit(solution)/shard_map/dot_general | solution.py:378
  105.5 4.9 reduce-scatter.7.cloned.1.call-done
  110.4 16.1 %moment.1 = f32[8,1024]{1,0:T(8,128)S(1)} custom-call(f32[8192,1024]{1,0:T(8,128)} %design.3, f32[64,128]{1,0:T(8,128)S(1)} %bitcast.32), custom_call_target="tpu_custom_call" | custom-call | flops 10000000000 | bytes 33554432 | tf_op jit(solution)/shard_map/moment/pallas_call | solution.py:306
  126.6 17.3 %shard_map.50 = f32[256,1024]{1,0:T(8,128)S(1)} custom-call(s32[1]{0:T(128)} %bitcast.1.base, f32[4096,256]{1,0:T(8,128)} %collective-permute-done.got, f32[8192,1024]{1,0:T(8,128)} %design.3), custom_call_target="tpu_custom_call" | custom-call | flops 2147483648 | bytes 20971520 | tf_op jit(solution)/shard_map/pallas_call | solution.py:351
  146.3 36.1 %reduce-scatter.9.cloned.1.call-done = f32[72,1024]{1,0:T(8,128)} async-done(((f32[576,1024]{1,0:T(8,128)}), f32[72,1024]{1,0:T(8,128)}) %reduce-scatter.9.cloned.1.call-update) | async-done | bytes 294928 | tf_op jit(solution)/shard_map/reduce_scatter | solution.py:381
  182.5 4.5 constant_dynamic-slice_fusion.3
  188.4 4.6 constant_dynamic-slice_fusion.2
  194.2 114.5 %collective-permute-done.1.got = f32[4096,256]{1,0:T(8,128)} collective-permute-done((f32[4096,256]{1,0:T(8,128)}, f32[4096,256]{1,0:T(8,128)}, u32[]{:S(2)}, u32[]{:S(2)}) %collective-permute-start.1) | collective-permute-done | bytes 4194336 | tf_op jit(solution)/shard_map/ppermute | solution.py:391
  308.6 18.4 %shard_map.51 = f32[256,1024]{1,0:T(8,128)} custom-call(s32[1]{0:T(128)} %bitcast.1.base, f32[4096,256]{1,0:T(8,128)} %collective-permute-done.1.got, f32[8192,1024]{1,0:T(8,128)} %design.3), custom_call_target="tpu_custom_call" | custom-call | flops 2147483648 | bytes 20971520 | tf_op jit(solution)/shard_map/pallas_call | solution.py:351
  327.2 24.8 %shard_map.52 = (f32[28,256,256]{2,1,0:T(8,128)}, f32[8,2,256,256]{3,2,1,0:T(8,128)S(1)}, f32[8,8,256]{2,1,0:T(8,128)S(1)}) custom-call(f32[1,1]{1,0:T(1,128)} %bitcast.25.refs_0_, f32[2,512,1024]{2,1,0:T(8,128)} %bitcast.53, f32[2,8,72,1024]{3,2,1,0:T(8,128)} %bitcast.48), custom_call_target="tpu_custom_call" | custom-call | flops 40000000000 | bytes 8388608 | tf_op jit(solution)/shard_map/pallas_call | solution.py:257
  357.7 39.6 %collective-permute-done.2.got = f32[4096,256]{1,0:T(8,128)} collective-permute-done((f32[4096,256]{1,0:T(8,128)}, f32[4096,256]{1,0:T(8,128)}, u32[]{:S(2)}, u32[]{:S(2)}) %collective-permute-start.2) | collective-permute-done | bytes 4194336 | tf_op jit(solution)/shard_map/ppermute | solution.py:391
  397.2 18.3 %shard_map.53 = f32[256,1024]{1,0:T(8,128)} custom-call(s32[1]{0:T(128)} %bitcast.1.base, f32[4096,256]{1,0:T(8,128)} %collective-permute-done.2.got, f32[8192,1024]{1,0:T(8,128)} %design.3), custom_call_target="tpu_custom_call" | custom-call | flops 2147483648 | bytes 20971520 | tf_op jit(solution)/shard_map/pallas_call | solution.py:351
  420.9 25.2 %reduce-scatter.13.cloned.1.call-done = f32[32,1024]{1,0:T(8,128)} async-done(((f32[256,1024]{1,0:T(8,128)}), f32[32,1024]{1,0:T(8,128)}) %reduce-scatter.13.cloned.1.call-update) | async-done | bytes 131088 | tf_op jit(solution)/shard_map/reduce_scatter | solution.py:381
  450.7 33.0 %all-gather.11.cloned.1.call-done = f32[512,1024]{1,0:T(8,128)} async-done(((f32[32,1024]{1,0:T(8,128)}), f32[512,1024]{1,0:T(8,128)}) %all-gather.11.cloned.1.call-update) | async-done | bytes 2097168 | tf_op jit(solution)/shard_map/all_gather | solution.py:384
  485.3 31.8 %shard_map.54 = (f32[28,256,256]{2,1,0:T(8,128)}, f32[8,2,256,256]{3,2,1,0:T(8,128)}, f32[8,8,256]{2,1,0:T(8,128)S(1)}) custom-call(f32[1,1]{1,0:T(1,128)} %bitcast.26.refs_0_, f32[2,512,1024]{2,1,0:T(8,128)} %bitcast.54, f32[2,8,72,1024]{3,2,1,0:T(8,128)} %bitcast.49, ...), custom_call_target="tpu_custom_call", output_to_operand_aliasing={{0}: (4, {}), {1}: (5, {}), {2}: (6, {})} | custom-call | flops 40000000000 | bytes 8388608 | tf_op jit(solution)/shard_map/pallas_call | solution.py:257
  517.1 13.6 %shard_map.56 = f32[128,1024]{1,0:T(8,128)} custom-call(s32[1]{0:T(128)} %bitcast.1.base, f32[4096,128]{1,0:T(8,128)} %collective-permute-done.3.got, f32[8192,1024]{1,0:T(8,128)} %design.3), custom_call_target="tpu_custom_call" | custom-call | flops 1073741824 | bytes 18874368 | tf_op jit(solution)/shard_map/pallas_call | solution.py:351
  534.0 41.7 %shard_map.55 = (f32[28,256,256]{2,1,0:T(8,128)}, f32[8,2,256,256]{3,2,1,0:T(8,128)}, f32[8,8,256]{2,1,0:T(8,128)S(1)}) custom-call(f32[1,1]{1,0:T(1,128)} %bitcast.27.refs_0_, f32[2,512,1024]{2,1,0:T(8,128)} %bitcast.55, f32[2,8,72,1024]{3,2,1,0:T(8,128)} %bitcast.50, ...), custom_call_target="tpu_custom_call", output_to_operand_aliasing={{0}: (5, {}), {1}: (6, {}), {2}: (7, {})} | custom-call | flops 40000000000 | bytes 8388608 | tf_op jit(solution)/shard_map/pallas_call | solution.py:257
  575.7 13.1 %shard_map.57 = f32[128,1024]{1,0:T(8,128)} custom-call(s32[1]{0:T(128)} %bitcast.1.base, f32[4096,128]{1,0:T(8,128)S(1)} %collective-permute-done.4.got, f32[8192,1024]{1,0:T(8,128)} %design.3), custom_call_target="tpu_custom_call" | custom-call | flops 1073741824 | bytes 18874368 | tf_op jit(solution)/shard_map/pallas_call | solution.py:351
  589.7 27.9 %reduce-scatter.17.cloned.1.call-done = f32[16,1024]{1,0:T(8,128)} async-done(((f32[128,1024]{1,0:T(8,128)}), f32[16,1024]{1,0:T(8,128)}) %reduce-scatter.17.cloned.1.call-update) | async-done | bytes 65552 | tf_op jit(solution)/shard_map/reduce_scatter | solution.py:381
  617.6 27.9 %all-gather.15.cloned.1.call-done = f32[256,1024]{1,0:T(8,128)} async-done(((f32[16,1024]{1,0:T(8,128)}), f32[256,1024]{1,0:T(8,128)}) %all-gather.15.cloned.1.call-update) | async-done | bytes 1048592 | tf_op jit(solution)/shard_map/all_gather | solution.py:384
  649.9 28.0 %shard_map.58 = (f32[28,256,256]{2,1,0:T(8,128)}, f32[8,2,256,256]{3,2,1,0:T(8,128)}, f32[8,8,256]{2,1,0:T(8,128)S(1)}) custom-call(f32[1,1]{1,0:T(1,128)} %bitcast.28.refs_0_, f32[2,512,1024]{2,1,0:T(8,128)} %bitcast.56, f32[2,8,72,1024]{3,2,1,0:T(8,128)} %bitcast.51, ...), custom_call_target="tpu_custom_call", output_to_operand_aliasing={{0}: (6, {}), {1}: (7, {}), {2}: (8, {})} | custom-call | flops 20000000000 | bytes 8388608 | tf_op jit(solution)/shard_map/pallas_call | solution.py:257
  679.2 33.4 %shard_map.59 = (f32[28,256,256]{2,1,0:T(8,128)}, f32[8,2,256,256]{3,2,1,0:T(8,128)}, f32[8,8,256]{2,1,0:T(8,128)S(1)}, f32[2,1024]{1,0:T(2,128)S(1)}) custom-call(f32[1,1]{1,0:T(1,128)} %bitcast.29.refs_0_, f32[2,512,1024]{2,1,0:T(8,128)} %bitcast.57, f32[2,8,72,1024]{3,2,1,0:T(8,128)} %bitcast.52, ...), custom_call_target="tpu_custom_call", output_to_operand_aliasing={{0}: (7, {}), {1}: (8, {}), {2}: (9, {})} | custom-call | flops 20000000000 | bytes 8388608 | tf_op jit(solution)/shard_map/pallas_call | solution.py:257
  712.7 16.1 %fit.1 = f32[64,128]{1,0:T(8,128)S(1)} custom-call(f32[8192,1024]{1,0:T(8,128)} %design.3, f32[1,1024]{1,0:T(1,128)S(1)} %constant_dynamic-slice_fusion.4.coeff), custom_call_target="tpu_custom_call" | custom-call | flops 10000000000 | bytes 33554432 | tf_op jit(solution)/shard_map/fit/pallas_call | solution.py:328
  (73 shorter events, 44.0 us)
Async XLA Ops:
  7.2 103.2 %reduce-scatter.7.cloned.1.call-start = ((), (), s32[]{:S(2)}) async-start(), calls=%async_computation.6 | async-start | bytes 2359296 | tf_op jit(solution)/shard_map/reduce_scatter | solution.py:381
  11.7 114.9 %collective-permute-start = (f32[4096,256]{1,0:T(8,128)}, f32[4096,256]{1,0:T(8,128)}, u32[]{:S(2)}, u32[]{:S(2)}) collective-permute-start(f32[4096,256]{1,0:T(8,128)} %constant_dynamic-slice_fusion.5), channel_id=1, source_target_pairs={{0,8},{8,0},{1,9},{9,1},{2,10},{10,2},{3,11},{11,3},{4,12},{12,4},... | collective-permute-start | bytes 12582920 | tf_op jit(solution)/shard_map/ppermute | solution.py:391
  74.7 107.7 %reduce-scatter.9.cloned.1.call-start = ((), (), s32[]{:S(2)}) async-start(), calls=%async_computation.8 | async-start | bytes 2654208 | tf_op jit(solution)/shard_map/reduce_scatter | solution.py:381
  74.7 35.7 %copy-start = (f32[8192]{0:T(1024)S(1)}, f32[8192]{0:T(1024)}, u32[]{:S(2)}) copy-start(f32[8192]{0:T(1024)} %param.4) | copy-start | bytes 98308
  145.5 181.6 %all-gather.7.cloned.1.call-start = ((), (), s32[]{:S(2)}) async-start(), calls=%async_computation.7 | async-start | bytes 4456448 | tf_op jit(solution)/shard_map/all_gather | solution.py:384
  146.3 180.9 %all-gather.9.cloned.1.call-start = ((), (), s32[]{:S(2)}) async-start(), calls=%async_computation.9 | async-start | bytes 5013504 | tf_op jit(solution)/shard_map/all_gather | solution.py:384
  182.4 175.2 %reduce-scatter.11.cloned.1.call-start = ((), (), s32[]{:S(2)}) async-start(), calls=%async_computation.10 | async-start | bytes 1179648 | tf_op jit(solution)/shard_map/reduce_scatter | solution.py:381
  187.0 121.7 %collective-permute-start.1 = (f32[4096,256]{1,0:T(8,128)}, f32[4096,256]{1,0:T(8,128)}, u32[]{:S(2)}, u32[]{:S(2)}) collective-permute-start(f32[4096,256]{1,0:T(8,128)} %constant_dynamic-slice_fusion.3), channel_id=1, source_target_pairs={{0,8},{8,0},{1,9},{9,1},{2,10},{10,2},{3,11},{11,3},{4,12},{12,4},... | collective-permute-start | bytes 12582920 | tf_op jit(solution)/shard_map/ppermute | solution.py:391
  193.1 204.2 %collective-permute-start.2 = (f32[4096,256]{1,0:T(8,128)}, f32[4096,256]{1,0:T(8,128)}, u32[]{:S(2)}, u32[]{:S(2)}) collective-permute-start(f32[4096,256]{1,0:T(8,128)} %constant_dynamic-slice_fusion.2), channel_id=1, source_target_pairs={{0,8},{8,0},{1,9},{9,1},{2,10},{10,2},{3,11},{11,3},{4,12},{12,4},... | collective-permute-start | bytes 12582920 | tf_op jit(solution)/shard_map/ppermute | solution.py:391
  327.1 119.0 %reduce-scatter.13.cloned.1.call-start = ((), (), s32[]{:S(2)}) async-start(), calls=%async_computation.12 | async-start | bytes 1179648 | tf_op jit(solution)/shard_map/reduce_scatter | solution.py:381
  352.0 1.9 copy-start.11
  415.5 68.2 %all-gather.11.cloned.1.call-start = ((), (), s32[]{:S(2)}) async-start(), calls=%async_computation.11 | async-start | bytes 2228224 | tf_op jit(solution)/shard_map/all_gather | solution.py:384
  416.3 114.5 %all-gather.13.cloned.1.call-start = ((), (), s32[]{:S(2)}) async-start(), calls=%async_computation.13 | async-start | bytes 2228224 | tf_op jit(solution)/shard_map/all_gather | solution.py:384
  419.4 97.7 %collective-permute-start.3 = (f32[4096,128]{1,0:T(8,128)}, f32[4096,128]{1,0:T(8,128)}, u32[]{:S(2)}, u32[]{:S(2)}) collective-permute-start(f32[4096,128]{1,0:T(8,128)} %constant_dynamic-slice_fusion.1), channel_id=1, source_target_pairs={{0,8},{8,0},{1,9},{9,1},{2,10},{10,2},{3,11},{11,3},{4,12},{12,4},... | collective-permute-start | bytes 6291464 | tf_op jit(solution)/shard_map/ppermute | solution.py:391
  446.1 129.6 %reduce-scatter.15.cloned.1.call-start = ((), (), s32[]{:S(2)}) async-start(), calls=%async_computation.14 | async-start | bytes 589824 | tf_op jit(solution)/shard_map/reduce_scatter | solution.py:381
  449.2 126.5 %collective-permute-start.4 = (f32[4096,128]{1,0:T(8,128)}, f32[4096,128]{1,0:T(8,128)S(1)}, u32[]{:S(2)}, u32[]{:S(2)}) collective-permute-start(f32[4096,128]{1,0:T(8,128)} %constant_dynamic-slice_fusion), channel_id=1, source_target_pairs={{0,8},{8,0},{1,9},{9,1},{2,10},{10,2},{3,11},{11,3},{4,12},{12,4},... | collective-permute-start | bytes 6291464 | tf_op jit(solution)/shard_map/ppermute | solution.py:391
  530.7 86.9 %reduce-scatter.17.cloned.1.call-start = ((), (), s32[]{:S(2)}) async-start(), calls=%async_computation.15 | async-start | bytes 589824 | tf_op jit(solution)/shard_map/reduce_scatter | solution.py:381
  530.8 1.6 copy-start.3
  588.9 56.6 %all-gather.15.cloned.1.call-start = ((), (), s32[]{:S(2)}) async-start(), calls=%async_computation.16 | async-start | bytes 1114112 | tf_op jit(solution)/shard_map/all_gather | solution.py:384
  589.6 88.3 %all-gather.17.cloned.1.call-start = ((), (), s32[]{:S(2)}) async-start(), calls=%async_computation.17 | async-start | bytes 1114112 | tf_op jit(solution)/shard_map/all_gather | solution.py:384
  649.9 28.1 %copy-start.5 = (f32[512,1024]{1,0:T(8,128)S(1)}, f32[512,1024]{1,0:T(8,128)}, u32[]{:S(2)}) copy-start(f32[512,1024]{1,0:T(8,128)} %all-gather.11.cloned.1.call-done) | copy-start | bytes 6291460
  649.9 28.1 %copy-start.9 = (f32[256,1024]{1,0:T(8,128)S(1)}, f32[256,1024]{1,0:T(8,128)}, u32[]{:S(2)}) copy-start(f32[256,1024]{1,0:T(8,128)} %all-gather.15.cloned.1.call-done) | copy-start | bytes 3145732
  712.6 20.0 %copy-start.1 = (f32[8192]{0:T(1024)S(1)}, f32[8192]{0:T(1024)}, u32[]{:S(2)}) copy-start(f32[8192]{0:T(1024)} %param.4) | copy-start | bytes 98308
  728.7 4.0 collective-permute-start.5
  (6 other events, 8.8 us)
Sparse Core Ops, SparseCore 0:
  74.8 35.5 reduce-scatter.6
  145.6 36.7 reduce-scatter.8
  184.7 48.7 all-gather.6
  235.5 52.0 all-gather.8
  327.2 30.4 reduce-scatter.10
  415.6 30.3 reduce-scatter.12
  448.3 35.3 all-gather.10
  486.0 35.5 all-gather.12
  530.8 28.4 reduce-scatter.14
  589.0 28.5 reduce-scatter.16
  619.8 25.5 all-gather.14
  647.6 25.6 all-gather.16

commit v3 on v2

--- a/solution.py
+++ b/solution.py
@@ -14,7 +14,9 @@
 BLK = 2 * SUB
 CHUNKS = (256, 256, 256, 128, 128)
 SWAP = ((0, 1), (1, 0))
+MESH = pl.DeviceIdType.MESH
 TILE = 512
+STREAM = 1024
 PACK = 32
 
 
@@ -305,9 +307,9 @@
     rows, cols = design.shape
     return pl.pallas_call(
         moment_kernel,
-        grid=(rows // TILE,),
+        grid=(rows // STREAM,),
         out_shape=jax.ShapeDtypeStruct((8, cols), jnp.float32),
-        in_specs=[pl.BlockSpec((TILE, cols), lambda i: (i, 0)), pl.BlockSpec((rows // SUB, SUB), lambda i: (0, 0))],
+        in_specs=[pl.BlockSpec((STREAM, cols), lambda i: (i, 0)), pl.BlockSpec((rows // SUB, SUB), lambda i: (0, 0))],
         out_specs=pl.BlockSpec((8, cols), lambda i: (0, 0)),
         scratch_shapes=[pltpu.VMEM((8, cols), jnp.float32)],
         compiler_params=pltpu.CompilerParams(vmem_limit_bytes=40 << 20),
@@ -327,9 +329,9 @@
     rows, cols = design.shape
     return pl.pallas_call(
         fit_kernel,
-        grid=(rows // TILE,),
+        grid=(rows // STREAM,),
         out_shape=jax.ShapeDtypeStruct((rows // SUB, SUB), jnp.float32),
-        in_specs=[pl.BlockSpec((TILE, cols), lambda i: (i, 0)), pl.BlockSpec((1, cols), lambda i: (0, 0))],
+        in_specs=[pl.BlockSpec((STREAM, cols), lambda i: (i, 0)), pl.BlockSpec((1, cols), lambda i: (0, 0))],
         out_specs=pl.BlockSpec((rows // SUB, SUB), lambda i: (0, 0)),
         compiler_params=pltpu.CompilerParams(vmem_limit_bytes=40 << 20),
         cost_estimate=pl.CostEstimate(flops=int(1e10), bytes_accessed=4 * rows * cols, transcendentals=0),
@@ -362,6 +364,51 @@
     )(base, got, design)
 
 
+def scatter_kernel(n, part, out, got, send, recv):
+    me = lax.axis_index("dp")
+    rows = out.shape[0]
+    barrier = pltpu.get_barrier_semaphore()
+    for t in range(1, n):
+        pl.semaphore_signal(barrier, inc=1, device_id={"dp": lax.rem(me + t, n)}, device_id_type=MESH)
+    pl.semaphore_wait(barrier, n - 1)
+    copies = []
+    for t in range(1, n):
+        peer = lax.rem(me + t, n)
+        copy = pltpu.make_async_remote_copy(
+            src_ref=part.at[pl.ds(pl.multiple_of(peer * rows, 8), rows)],
+            dst_ref=got.at[t - 1],
+            send_sem=send.at[t - 1],
+            recv_sem=recv.at[t - 1],
+            device_id={"dp": peer},
+            device_id_type=MESH,
+        )
+        copy.start()
+        copies.append(copy)
+    out[...] = part[pl.ds(pl.multiple_of(me * rows, 8), rows), :]
+    for t in range(1, n):
+        copies[t - 1].wait_recv()
+        out[...] += got[t - 1]
+    for copy in copies:
+        copy.wait_send()
+
+
+def scatter_call(n, ident, part):
+    rows, cols = part.shape[0] // n, part.shape[1]
+    return pl.pallas_call(
+        functools.partial(scatter_kernel, n),
+        out_shape=jax.ShapeDtypeStruct((rows, cols), jnp.float32),
+        in_specs=[pl.BlockSpec(memory_space=pltpu.VMEM)],
+        out_specs=pl.BlockSpec(memory_space=pltpu.VMEM),
+        scratch_shapes=[
+            pltpu.VMEM((n - 1, rows, cols), jnp.float32),
+            pltpu.SemaphoreType.DMA((n - 1,)),
+            pltpu.SemaphoreType.DMA((n - 1,)),
+        ],
+        compiler_params=pltpu.CompilerParams(collective_id=ident, has_side_effects=True, vmem_limit_bytes=24 << 20),
+        cost_estimate=pl.CostEstimate(flops=int(1e10), bytes_accessed=16 * rows * cols, transcendentals=0),
+    )(part)
+
+
 def after(value, *deps):
     return lax.optimization_barrier((value, *deps))[0]
 
@@ -403,7 +450,7 @@
             return cross_call(after(base, *deps), arrived[n], design)
 
         mixed = cross(0, moment).reshape(groups, CHUNKS[0] // groups, cols)
-        rest_rs = scatter(jnp.concatenate([rest, moment, mixed], axis=1).reshape(-1, cols))
+        rest_rs = scatter_call(groups, 0, jnp.concatenate([rest, moment, mixed], axis=1).reshape(-1, cols))
 
         source = []
         for n, width in enumerate(CHUNKS):
@@ -418,20 +465,20 @@
                 after(lam, *deps), top, rest, ccs[:n], state,
             )
 
-        rs1 = scatter(cross(1, rest_rs))
+        rs1 = scatter_call(groups, 1, cross(1, rest_rs))
         rest = gather(rest_rs).reshape(2, groups, -1, cols)
-        state, _ = factor(0, None)
-        rs2 = scatter(cross(2, *state, rs1))
         ccs.append(gather(rs1))
+        state, _ = factor(0, None, rs1)
         state, _ = factor(1, state)
-        rs3 = scatter(cross(3, *state, rs2))
+        rs2 = scatter_call(groups, 2, cross(2, *state))
         ccs.append(gather(rs2))
-        state, _ = factor(2, state)
-        rs4 = scatter(cross(4, *state, rs3))
+        rs3 = scatter_call(groups, 3, cross(3, rs2))
         ccs.append(gather(rs3))
-        state, _ = factor(3, state)
+        state, _ = factor(2, state, rs3)
+        rs4 = scatter_call(groups, 4, cross(4, *state))
         ccs.append(gather(rs4))
-        _, coeff = factor(4, state, rs4)
+        state, _ = factor(3, state, rs4)
+        _, coeff = factor(4, state)
 
         mine = lax.dynamic_slice_in_dim(coeff, side, 1)
         fit = fit_call(design, mine)

time: 751 us -> 790 us (1.052)
  Pallas kernels: 273 us -> 339 us
  waiting for transfers between devices: 317 us -> 294 us
    ppermute x5, waiting for transfers between devices: 154 us -> 250 us  [local_fit(): arrived.append(lax.ppermute(piece, 'tp', SWAP))]
    pallas_call x2 -> x7, Pallas kernels: 32.2 us -> 103 us  [the longest x5 78 us: scatter_call(): pl.pallas_call(functools.partial(scatter_kernel, n), out_shape=jax.ShapeD...]
    reduce_scatter x6 -> x1, waiting for transfers between devices: 97.8 us -> 38.4 us  [scatter(): return lax.psum_scatter(partial, 'dp', scatter_dimension=0, tiled=True)]
    all_gather x6, waiting for transfers between devices: 61 us -> 3.66 us  [gather(): lax.all_gather(mine, ('tp', 'dp'), axis=0, tiled=True).reshape(2, -1, cols)]
  transfers between devices with their start and end apart: 18 -> 13, of which waited for: 10 -> 7; matrix products, arithmetic and copies ran while one was open for 14% -> 7% of each run, Pallas kernels for 24% -> 34%
where the time goes in v3:
time: 790 us; the launch traced here: 779 us
  Pallas kernels  339 us (43%)
  waiting for transfers between devices  294 us (37%)
  matrix products  90.5 us (11%)
  local copies, waits for them, and re-layouts  31 us (4%)
  between operations  15.5 us (2%)
  starting transfers between devices  8.15 us (1%)
    ppermute x5, waiting for transfers between devices, local_fit(): arrived.append(lax.ppermute(piece, 'tp', SWAP))  250 us
    pallas_call x5, Pallas kernels, factor_call(): pl.pallas_call(functools.partial(factor_kernel, first, steps, source, las...  159 us
    dot_general x2, matrix products, gram_of(): lax.dot_general(lhs, rhs, CONTRACT_ROWS, precision=HIGHEST, preferred_ele...  90.5 us
    pallas_call x5, Pallas kernels, scatter_call(): pl.pallas_call(functools.partial(scatter_kernel, n), out_shape=jax.ShapeD...  78 us
    pallas_call x5, Pallas kernels, cross_call(): pl.pallas_call(cross_kernel, grid_spec=pltpu.PrefetchScalarGridSpec(num_s...  77 us
    reduce_scatter x1, waiting for transfers between devices, scatter(): return lax.psum_scatter(partial, 'dp', scatter_dimension=0, tiled=True)  38.4 us
    dynamic_slice x5, local copies, waits for them, and re-layouts, local_fit(): piece = lax.dynamic_slice(design, (offset, at), (part, width))  19.6 us
  transfers between devices with their start and end apart: 13, of which 7 were waited for; matrix products, arithmetic and copies ran while one was open for 7% of the time, Pallas kernels for 34%

profile of v3, /device:TPU:0, one launch (start us, length us, event | category | flops | bytes accessed | tf_op | source)
XLA Modules:
  0.0 779.5 jit_solution(10164695675824655865)
XLA Ops:
  7.2 59.6 %fusion.3 = f32[512,1024]{1,0:T(8,128)} fusion(f32[8192,1024]{1,0:T(8,128)} %design.3), kind=kOutput, calls=%fused_computation.3 | convolution fusion | flops 51539607552 | bytes 52428800 | tf_op jit(solution)/shard_map/dot_general | solution.py:425
  66.9 38.4 %reduce-scatter.2.cloned.1.call-done = f32[64,1024]{1,0:T(8,128)} async-done(((f32[512,1024]{1,0:T(8,128)}), f32[64,1024]{1,0:T(8,128)}) %reduce-scatter.2.cloned.1.call-update) | async-done | bytes 262160 | tf_op jit(solution)/shard_map/reduce_scatter | solution.py:428
  111.3 30.9 %fusion = f32[512,512]{1,0:T(8,128)S(1)} fusion(f32[8192,1024]{1,0:T(8,128)} %design.3), kind=kOutput, calls=%fused_computation | convolution fusion | flops 25769803776 | bytes 34603008 | tf_op jit(solution)/shard_map/dot_general | solution.py:425
  142.3 12.3 %moment.1 = f32[8,1024]{1,0:T(8,128)S(1)} custom-call(f32[8192,1024]{1,0:T(8,128)} %design.3, f32[64,128]{1,0:T(8,128)S(1)} %bitcast.33), custom_call_target="tpu_custom_call" | custom-call | flops 10000000000 | bytes 33554432 | tf_op jit(solution)/shard_map/moment/pallas_call | solution.py:308
  154.7 60.7 %collective-permute-done.got = f32[4096,256]{1,0:T(8,128)} collective-permute-done((f32[4096,256]{1,0:T(8,128)}, f32[4096,256]{1,0:T(8,128)}, u32[]{:S(2)}, u32[]{:S(2)}) %collective-permute-start) | collective-permute-done | bytes 4194336 | tf_op jit(solution)/shard_map/ppermute | solution.py:438
  215.4 17.2 %shard_map.50 = f32[256,1024]{1,0:T(8,128)S(1)} custom-call(s32[1]{0:T(128)} %bitcast.6.base, f32[4096,256]{1,0:T(8,128)} %collective-permute-done.got, f32[8192,1024]{1,0:T(8,128)} %design.3), custom_call_target="tpu_custom_call" | custom-call | flops 2147483648 | bytes 20971520 | tf_op jit(solution)/shard_map/pallas_call | solution.py:353
  232.9 28.2 %shard_map.51 = f32[72,1024]{1,0:T(8,128)} custom-call(f32[576,1024]{1,0:T(8,128)S(1)} %bitcast.31), custom_call_target="tpu_custom_call" | custom-call | flops 10000000000 | bytes 1179648 | tf_op jit(solution)/shard_map/pallas_call | solution.py:397
  267.1 106.2 %collective-permute-done.1.got = f32[4096,256]{1,0:T(8,128)} collective-permute-done((f32[4096,256]{1,0:T(8,128)}, f32[4096,256]{1,0:T(8,128)}, u32[]{:S(2)}, u32[]{:S(2)}) %collective-permute-start.1) | collective-permute-done | bytes 4194336 | tf_op jit(solution)/shard_map/ppermute | solution.py:438
  373.3 17.4 %shard_map.52.part = f32[256,1024]{1,0:T(8,128)S(1)} custom-call(s32[1]{0:T(128)} %bitcast.6.base, f32[4096,256]{1,0:T(8,128)} %collective-permute-done.1.got, f32[8192,1024]{1,0:T(8,128)} %design.3), custom_call_target="tpu_custom_call" | custom-call | flops 2147483648 | bytes 20971520 | tf_op jit(solution)/shard_map/pallas_call | solution.py:353
  390.7 14.8 %shard_map.53 = f32[32,1024]{1,0:T(8,128)} custom-call(f32[256,1024]{1,0:T(8,128)S(1)} %shard_map.52.part), custom_call_target="tpu_custom_call" | custom-call | flops 10000000000 | bytes 524288 | tf_op jit(solution)/shard_map/pallas_call | solution.py:397
  412.3 24.8 %shard_map.54 = (f32[28,256,256]{2,1,0:T(8,128)}, f32[8,2,256,256]{3,2,1,0:T(8,128)S(1)}, f32[8,8,256]{2,1,0:T(8,128)S(1)}) custom-call(f32[1,1]{1,0:T(1,128)} %bitcast.27.refs_0_, f32[2,512,1024]{2,1,0:T(8,128)} %bitcast.53, f32[2,8,72,1024]{3,2,1,0:T(8,128)} %bitcast.48), custom_call_target="tpu_custom_call" | custom-call | flops 40000000000 | bytes 8388608 | tf_op jit(solution)/shard_map/pallas_call | solution.py:259
  444.2 31.7 %shard_map.55 = (f32[28,256,256]{2,1,0:T(8,128)}, f32[8,2,256,256]{3,2,1,0:T(8,128)}, f32[8,8,256]{2,1,0:T(8,128)S(1)}) custom-call(f32[1,1]{1,0:T(1,128)} %bitcast.25.refs_0_, f32[2,512,1024]{2,1,0:T(8,128)} %bitcast.54, f32[2,8,72,1024]{3,2,1,0:T(8,128)} %bitcast.49, ...), custom_call_target="tpu_custom_call", output_to_operand_aliasing={{0}: (4, {}), {1}: (5, {}), {2}: (6, {})} | custom-call | flops 40000000000 | bytes 8388608 | tf_op jit(solution)/shard_map/pallas_call | solution.py:259
  475.9 33.7 %collective-permute-done.2.got = f32[4096,256]{1,0:T(8,128)} collective-permute-done((f32[4096,256]{1,0:T(8,128)}, f32[4096,256]{1,0:T(8,128)}, u32[]{:S(2)}, u32[]{:S(2)}) %collective-permute-start.2) | collective-permute-done | bytes 4194336 | tf_op jit(solution)/shard_map/ppermute | solution.py:438
  509.6 17.2 %shard_map.56.part = f32[256,1024]{1,0:T(8,128)S(1)} custom-call(s32[1]{0:T(128)} %bitcast.6.base, f32[4096,256]{1,0:T(8,128)} %collective-permute-done.2.got, f32[8192,1024]{1,0:T(8,128)} %design.3), custom_call_target="tpu_custom_call" | custom-call | flops 2147483648 | bytes 20971520 | tf_op jit(solution)/shard_map/pallas_call | solution.py:353
  526.9 14.8 %shard_map.57 = f32[32,1024]{1,0:T(8,128)} custom-call(f32[256,1024]{1,0:T(8,128)S(1)} %shard_map.56.part), custom_call_target="tpu_custom_call" | custom-call | flops 10000000000 | bytes 524288 | tf_op jit(solution)/shard_map/pallas_call | solution.py:397
  549.9 49.5 %collective-permute-done.3.got = f32[4096,128]{1,0:T(8,128)} collective-permute-done((f32[4096,128]{1,0:T(8,128)}, f32[4096,128]{1,0:T(8,128)}, u32[]{:S(2)}, u32[]{:S(2)}) %collective-permute-start.3) | collective-permute-done | bytes 2097184 | tf_op jit(solution)/shard_map/ppermute | solution.py:438
  599.4 12.8 %shard_map.58.part = f32[128,1024]{1,0:T(8,128)S(1)} custom-call(s32[1]{0:T(128)} %bitcast.6.base, f32[4096,128]{1,0:T(8,128)} %collective-permute-done.3.got, f32[8192,1024]{1,0:T(8,128)} %design.3), custom_call_target="tpu_custom_call" | custom-call | flops 1073741824 | bytes 18874368 | tf_op jit(solution)/shard_map/pallas_call | solution.py:353
  612.2 10.3 %shard_map.59 = f32[16,1024]{1,0:T(8,128)} custom-call(f32[128,1024]{1,0:T(8,128)S(1)} %shard_map.58.part), custom_call_target="tpu_custom_call" | custom-call | flops 10000000000 | bytes 262144 | tf_op jit(solution)/shard_map/pallas_call | solution.py:397
  625.8 41.6 %shard_map.60 = (f32[28,256,256]{2,1,0:T(8,128)}, f32[8,2,256,256]{3,2,1,0:T(8,128)}, f32[8,8,256]{2,1,0:T(8,128)S(1)}) custom-call(f32[1,1]{1,0:T(1,128)} %bitcast.28.refs_0_, f32[2,512,1024]{2,1,0:T(8,128)} %bitcast.55, f32[2,8,72,1024]{3,2,1,0:T(8,128)} %bitcast.50, ...), custom_call_target="tpu_custom_call", output_to_operand_aliasing={{0}: (5, {}), {1}: (6, {}), {2}: (7, {})} | custom-call | flops 40000000000 | bytes 8388608 | tf_op jit(solution)/shard_map/pallas_call | solution.py:259
  667.4 12.4 %shard_map.61.part = f32[128,1024]{1,0:T(8,128)S(1)} custom-call(s32[1]{0:T(128)} %bitcast.6.base, f32[4096,128]{1,0:T(8,128)S(1)} %collective-permute-done.4.got, f32[8192,1024]{1,0:T(8,128)} %design.3), custom_call_target="tpu_custom_call" | custom-call | flops 1073741824 | bytes 18874368 | tf_op jit(solution)/shard_map/pallas_call | solution.py:353
  679.8 10.0 %shard_map.62 = f32[16,1024]{1,0:T(8,128)} custom-call(f32[128,1024]{1,0:T(8,128)S(1)} %shard_map.61.part), custom_call_target="tpu_custom_call" | custom-call | flops 10000000000 | bytes 262144 | tf_op jit(solution)/shard_map/pallas_call | solution.py:397
  692.6 28.0 %shard_map.63 = (f32[28,256,256]{2,1,0:T(8,128)}, f32[8,2,256,256]{3,2,1,0:T(8,128)}, f32[8,8,256]{2,1,0:T(8,128)S(1)}) custom-call(f32[1,1]{1,0:T(1,128)} %bitcast.29.refs_0_, f32[2,512,1024]{2,1,0:T(8,128)} %bitcast.56, f32[2,8,72,1024]{3,2,1,0:T(8,128)} %bitcast.51, ...), custom_call_target="tpu_custom_call", output_to_operand_aliasing={{0}: (6, {}), {1}: (7, {}), {2}: (8, {})} | custom-call | flops 20000000000 | bytes 8388608 | tf_op jit(solution)/shard_map/pallas_call | solution.py:259
  721.9 33.4 %shard_map.64 = (f32[28,256,256]{2,1,0:T(8,128)}, f32[8,2,256,256]{3,2,1,0:T(8,128)}, f32[8,8,256]{2,1,0:T(8,128)S(1)}, f32[2,1024]{1,0:T(2,128)S(1)}) custom-call(f32[1,1]{1,0:T(1,128)} %bitcast.26.refs_0_, f32[2,512,1024]{2,1,0:T(8,128)} %bitcast.57, f32[2,8,72,1024]{3,2,1,0:T(8,128)} %bitcast.52, ...), custom_call_target="tpu_custom_call", output_to_operand_aliasing={{0}: (7, {}), {1}: (8, {}), {2}: (9, {})} | custom-call | flops 20000000000 | bytes 8388608 | tf_op jit(solution)/shard_map/pallas_call | solution.py:259
  755.4 12.2 %fit.1 = f32[64,128]{1,0:T(8,128)S(1)} custom-call(f32[8192,1024]{1,0:T(8,128)} %design.3, f32[1,1024]{1,0:T(1,128)S(1)} %constant_dynamic-slice_fusion.4.coeff), custom_call_target="tpu_custom_call" | custom-call | flops 10000000000 | bytes 33554432 | tf_op jit(solution)/shard_map/fit/pallas_call | solution.py:330
  (61 shorter events, 45.9 us)
Async XLA Ops:
  7.2 98.1 %reduce-scatter.2.cloned.1.call-start = ((), (), s32[]{:S(2)}) async-start(), calls=%async_computation.1 | async-start | bytes 2359296 | tf_op jit(solution)/shard_map/reduce_scatter | solution.py:428
  66.8 345.4 %all-gather.7.cloned.1.call-start = ((), (), s32[]{:S(2)}) async-start(), calls=%async_computation.2 | async-start | bytes 4456448 | tf_op jit(solution)/shard_map/all_gather | solution.py:431
  105.3 307.0 %all-gather.9.cloned.1.call-start = ((), (), s32[]{:S(2)}) async-start(), calls=%async_computation.3 | async-start | bytes 5013504 | tf_op jit(solution)/shard_map/all_gather | solution.py:431
  109.8 105.6 %collective-permute-start = (f32[4096,256]{1,0:T(8,128)}, f32[4096,256]{1,0:T(8,128)}, u32[]{:S(2)}, u32[]{:S(2)}) collective-permute-start(f32[4096,256]{1,0:T(8,128)} %constant_dynamic-slice_fusion.5), channel_id=1, source_target_pairs={{0,8},{8,0},{1,9},{9,1},{2,10},{10,2},{3,11},{11,3},{4,12},{12,4},... | collective-permute-start | bytes 12582920 | tf_op jit(solution)/shard_map/ppermute | solution.py:438
  111.3 31.1 %copy-start = (f32[8192]{0:T(1024)S(1)}, f32[8192]{0:T(1024)}, u32[]{:S(2)}) copy-start(f32[8192]{0:T(1024)} %param.4) | copy-start | bytes 98308
  261.1 181.5 %all-gather.11.cloned.1.call-start = ((), (), s32[]{:S(2)}) async-start(), calls=%async_computation.4 | async-start | bytes 2228224 | tf_op jit(solution)/shard_map/all_gather | solution.py:431
  265.6 107.7 %collective-permute-start.1 = (f32[4096,256]{1,0:T(8,128)}, f32[4096,256]{1,0:T(8,128)}, u32[]{:S(2)}, u32[]{:S(2)}) collective-permute-start(f32[4096,256]{1,0:T(8,128)} %constant_dynamic-slice_fusion.3), channel_id=1, source_target_pairs={{0,8},{8,0},{1,9},{9,1},{2,10},{10,2},{3,11},{11,3},{4,12},{12,4},... | collective-permute-start | bytes 12582920 | tf_op jit(solution)/shard_map/ppermute | solution.py:438
  405.6 217.0 %all-gather.13.cloned.1.call-start = ((), (), s32[]{:S(2)}) async-start(), calls=%async_computation.5 | async-start | bytes 2228224 | tf_op jit(solution)/shard_map/all_gather | solution.py:431
  410.1 99.5 %collective-permute-start.2 = (f32[4096,256]{1,0:T(8,128)}, f32[4096,256]{1,0:T(8,128)}, u32[]{:S(2)}, u32[]{:S(2)}) collective-permute-start(f32[4096,256]{1,0:T(8,128)} %constant_dynamic-slice_fusion.2), channel_id=1, source_target_pairs={{0,8},{8,0},{1,9},{9,1},{2,10},{10,2},{3,11},{11,3},{4,12},{12,4},... | collective-permute-start | bytes 12582920 | tf_op jit(solution)/shard_map/ppermute | solution.py:438
  437.1 2.0 copy-start.10
  442.6 1.6 copy-start.2
  541.7 148.1 %all-gather.15.cloned.1.call-start = ((), (), s32[]{:S(2)}) async-start(), calls=%async_computation.6 | async-start | bytes 1114112 | tf_op jit(solution)/shard_map/all_gather | solution.py:431
  544.8 54.6 %collective-permute-start.3 = (f32[4096,128]{1,0:T(8,128)}, f32[4096,128]{1,0:T(8,128)}, u32[]{:S(2)}, u32[]{:S(2)}) collective-permute-start(f32[4096,128]{1,0:T(8,128)} %constant_dynamic-slice_fusion.1), channel_id=1, source_target_pairs={{0,8},{8,0},{1,9},{9,1},{2,10},{10,2},{3,11},{11,3},{4,12},{12,4},... | collective-permute-start | bytes 6291464 | tf_op jit(solution)/shard_map/ppermute | solution.py:438
  549.3 118.1 %collective-permute-start.4 = (f32[4096,128]{1,0:T(8,128)}, f32[4096,128]{1,0:T(8,128)S(1)}, u32[]{:S(2)}, u32[]{:S(2)}) collective-permute-start(f32[4096,128]{1,0:T(8,128)} %constant_dynamic-slice_fusion), channel_id=1, source_target_pairs={{0,8},{8,0},{1,9},{9,1},{2,10},{10,2},{3,11},{11,3},{4,12},{12,4},... | collective-permute-start | bytes 6291464 | tf_op jit(solution)/shard_map/ppermute | solution.py:438
  622.5 98.1 %all-gather.17.cloned.1.call-start = ((), (), s32[]{:S(2)}) async-start(), calls=%async_computation.7 | async-start | bytes 1114112 | tf_op jit(solution)/shard_map/all_gather | solution.py:431
  622.6 1.6 copy-start.3
  624.2 1.6 copy-start.5
  679.8 10.0 %copy-start.4 = (f32[512,1024]{1,0:T(8,128)S(1)}, f32[512,1024]{1,0:T(8,128)}, u32[]{:S(2)}) copy-start(f32[512,1024]{1,0:T(8,128)} %all-gather.11.cloned.1.call-done) | copy-start | bytes 6291460
  689.8 1.6 copy-start.6
  691.4 1.2 copy-start.7
  692.6 28.0 %copy-start.8 = (f32[256,1024]{1,0:T(8,128)S(1)}, f32[256,1024]{1,0:T(8,128)}, u32[]{:S(2)}) copy-start(f32[256,1024]{1,0:T(8,128)} %all-gather.15.cloned.1.call-done) | copy-start | bytes 3145732
  720.7 1.2 copy-start.9
  755.4 16.3 %copy-start.1 = (f32[8192]{0:T(1024)S(1)}, f32[8192]{0:T(1024)}, u32[]{:S(2)}) copy-start(f32[8192]{0:T(1024)} %param.4) | copy-start | bytes 98308
  767.5 4.1 collective-permute-start.5
Sparse Core Ops, SparseCore 0:
  66.9 38.2 reduce-scatter.1
  107.5 48.7 all-gather.6
  261.2 53.4 all-gather.8
  405.7 36.8 all-gather.10
  541.8 36.7 all-gather.12
  622.6 27.4 all-gather.14
  689.9 26.0 all-gather.16

commit v4 on v3

--- a/solution.py
+++ b/solution.py
@@ -28,45 +28,44 @@
     return (i * (i - 1)) // 2 + j
 
 
-def eliminate(rows, aug, put):
+def eliminate(rows, put):
     sub = lax.broadcasted_iota(jnp.int32, (8, SUB), 0)
+    lane = lax.broadcasted_iota(jnp.int32, (8, SUB), 1)
     full = lambda x: jnp.broadcast_to(x, (8, SUB))
 
     def octet(low, m, carry):
         pick = lambda x, c: jnp.take_along_axis(x, jnp.full((8, SUB), 8 * m + c, jnp.int32), axis=1, mode="promise_in_bounds")
-        at = pl.ds(pl.multiple_of(8 * m, 8), 8)
-        row, add = rows[at, :], aug[at, :]
-        diag = [pick(row, c) for c in range(8)]
+        row = rows[pl.ds(pl.multiple_of(8 * m, 8), 8), :]
         spans = [slice(8 * v, 8 * v + 8) for v in range(low + 1, SUB // 8)]
-        cols = [[pick(rows[span, :], c) for c in range(8)] for span in spans]
-        piv_rows, aug_rows, recips, links = [], [], [], []
+        picks = [[pick(x, c) for x in [row, *(rows[span, :] for span in spans)]] for c in range(8)]
+        diag = [picks[c][0] for c in range(8)]
+        cols = [[picks[c][n + 1] for c in range(8)] for n in range(len(spans))]
+        inside = (lane >= 8 * m) & (lane < 8 * m + 8)
+        row = jnp.where(inside, jnp.where(lane - 8 * m == sub, 1.0, 0.0).astype(jnp.float32), row)
+        scaled, links = [], []
         pivots = jnp.ones((8, SUB), jnp.float32)
         for j in range(8):
             pivot = full(diag[j][j : j + 1, :])
             recip = 1.0 / pivot
             pivots = jnp.where(sub == j, pivot, pivots)
             mult = jnp.where(sub > j, diag[j] * recip, 0.0)
-            pr, ar = full(row[j : j + 1, :]), full(add[j : j + 1, :])
-            row, add = row - mult * pr, add - mult * ar
+            pivot_row = full(row[j : j + 1, :])
+            scaled.append(pivot_row * recip)
+            row = row - mult * pivot_row
             link = {}
             for c in range(j + 1, 8):
-                link[c] = full(diag[c][j : j + 1, :])
-                diag[c] = diag[c] - mult * link[c]
-            piv_rows.append(pr)
-            aug_rows.append(ar)
-            recips.append(recip)
+                head = full(diag[c][j : j + 1, :])
+                link[c] = head * recip
+                diag[c] = diag[c] - mult * head
             links.append(link)
-        put(m, add * lax.rsqrt(pivots))
+        put(m, jnp.where(lane < 8 * m + 8, row * lax.rsqrt(pivots), 0.0))
         for span, col in zip(spans, cols):
-            r, e = rows[span, :], aug[span, :]
+            r = jnp.where(inside, 0.0, rows[span, :])
             for j in range(8):
-                mult = col[j] * recips[j]
-                r = r - mult * piv_rows[j]
-                e = e - mult * aug_rows[j]
+                r = r - col[j] * scaled[j]
                 for c in range(j + 1, 8):
-                    col[c] = col[c] - mult * links[j][c]
+                    col[c] = col[c] - col[j] * links[j][c]
             rows[span, :] = r
-            aug[span, :] = e
         return carry
 
     for low in range(0, SUB // 8, 4):
@@ -83,7 +82,7 @@
     refs = refs[3:]
     if last:
         x_ref, refs = refs[0], refs[1:]
-    low, inv, half, diag, cross, prev, mom, panel, work, acc, up, rows, aug, sems, wsems = refs
+    low, inv, half, diag, cross, prev, mom, panel, work, acc, up, rows, sems, wsems = refs
     end = first + steps
     width = SUB * steps
     loads = []
@@ -168,12 +167,11 @@
         def factor(b, carry):
             at = pl.ds(pl.multiple_of(b * SUB, SUB), SUB)
             rows[...] = work[at, at]
-            aug[...] = jnp.where(eye, 1.0, 0.0).astype(jnp.float32)
 
             def put(m, block):
                 inv[k, 0, pl.ds(pl.multiple_of(b * SUB + 8 * m, 8), 8), at] = block
 
-            eliminate(rows, aug, put)
+            eliminate(rows, put)
 
             @pl.when(b == 0)
             def _():
@@ -275,7 +273,6 @@
             pltpu.VMEM((n_blocks, 8, BLK), jnp.float32),
             pltpu.VMEM((SUB, SUB), jnp.float32),
             pltpu.VMEM((SUB, SUB), jnp.float32),
-            pltpu.VMEM((SUB, SUB), jnp.float32),
             pltpu.SemaphoreType.DMA((80,)),
             pltpu.SemaphoreType.DMA((4,)),
         ],
@@ -364,31 +361,47 @@
     )(base, got, design)
 
 
-def scatter_kernel(n, part, out, got, send, recv):
+def scatter_kernel(n, part, out, near, sums, got, near_send, near_recv, send, recv):
     me = lax.axis_index("dp")
     rows = out.shape[0]
+    chips = n // 2
+    core, chip = lax.rem(me, 2), me // 2
+    twin = me + 1 - 2 * core
+    peers = [2 * lax.rem(chip + t, chips) + core for t in range(1, chips)]
     barrier = pltpu.get_barrier_semaphore()
-    for t in range(1, n):
-        pl.semaphore_signal(barrier, inc=1, device_id={"dp": lax.rem(me + t, n)}, device_id_type=MESH)
-    pl.semaphore_wait(barrier, n - 1)
-    copies = []
-    for t in range(1, n):
-        peer = lax.rem(me + t, n)
+    for peer in [twin, *peers]:
+        pl.semaphore_signal(barrier, inc=1, device_id={"dp": peer}, device_id_type=MESH)
+    pl.semaphore_wait(barrier, chips)
+
+    def piece(t, side):
+        return part.at[pl.ds(pl.multiple_of((2 * lax.rem(chip + t, chips) + side) * rows, 8), rows)]
+
+    first, second = [], []
+    order = [*range(1, chips), 0]
+    for t in order:
         copy = pltpu.make_async_remote_copy(
-            src_ref=part.at[pl.ds(pl.multiple_of(peer * rows, 8), rows)],
-            dst_ref=got.at[t - 1],
-            send_sem=send.at[t - 1],
-            recv_sem=recv.at[t - 1],
-            device_id={"dp": peer},
-            device_id_type=MESH,
+            src_ref=piece(t, 1 - core), dst_ref=near.at[t], send_sem=near_send.at[t], recv_sem=near_recv.at[t],
+            device_id={"dp": twin}, device_id_type=MESH,
         )
         copy.start()
-        copies.append(copy)
-    out[...] = part[pl.ds(pl.multiple_of(me * rows, 8), rows), :]
-    for t in range(1, n):
-        copies[t - 1].wait_recv()
-        out[...] += got[t - 1]
-    for copy in copies:
+        first.append(copy)
+    for t, copy in zip(order, first):
+        copy.wait_recv()
+        total = piece(t, core)[...] + near[t]
+        if t == 0:
+            out[...] = total
+            continue
+        sums[t - 1] = total
+        copy = pltpu.make_async_remote_copy(
+            src_ref=sums.at[t - 1], dst_ref=got.at[t - 1], send_sem=send.at[t - 1], recv_sem=recv.at[t - 1],
+            device_id={"dp": peers[t - 1]}, device_id_type=MESH,
+        )
+        copy.start()
+        second.append(copy)
+    for t, copy in enumerate(second):
+        copy.wait_recv()
+        out[...] += got[t]
+    for copy in [*first, *second]:
         copy.wait_send()
 
 
@@ -400,9 +413,13 @@
         in_specs=[pl.BlockSpec(memory_space=pltpu.VMEM)],
         out_specs=pl.BlockSpec(memory_space=pltpu.VMEM),
         scratch_shapes=[
-            pltpu.VMEM((n - 1, rows, cols), jnp.float32),
-            pltpu.SemaphoreType.DMA((n - 1,)),
-            pltpu.SemaphoreType.DMA((n - 1,)),
+            pltpu.VMEM((n // 2, rows, cols), jnp.float32),
+            pltpu.VMEM((n // 2 - 1, rows, cols), jnp.float32),
+            pltpu.VMEM((n // 2 - 1, rows, cols), jnp.float32),
+            pltpu.SemaphoreType.DMA((n // 2,)),
+            pltpu.SemaphoreType.DMA((n // 2,)),
+            pltpu.SemaphoreType.DMA((n // 2 - 1,)),
+            pltpu.SemaphoreType.DMA((n // 2 - 1,)),
         ],
         compiler_params=pltpu.CompilerParams(collective_id=ident, has_side_effects=True, vmem_limit_bytes=24 << 20),
         cost_estimate=pl.CostEstimate(flops=int(1e10), bytes_accessed=16 * rows * cols, transcendentals=0),

time: 790 us -> 760 us (0.962)
  Pallas kernels: 339 us -> 300 us
  waiting for transfers between devices: 294 us -> 303 us
    pallas_call x5, Pallas kernels: 78 us -> 56.1 us  [scatter_call(): pl.pallas_call(functools.partial(scatter_kernel, n), out_shape=jax.ShapeD...]
    pallas_call x5, Pallas kernels: 159 us -> 143 us  [factor_call(): pl.pallas_call(functools.partial(factor_kernel, first, steps, source, las...]
  transfers between devices with their start and end apart: 13 -> 13, of which waited for: 7 -> 7; matrix products, arithmetic and copies ran while one was open for 7% -> 7% of each run, Pallas kernels for 34% -> 31%
where the time goes in v4:
time: 760 us; the launch traced here: 750 us
  waiting for transfers between devices  303 us (40%)
  Pallas kernels  300 us (39%)
  matrix products  90.3 us (12%)
  local copies, waits for them, and re-layouts  31 us (4%)
  between operations  15.5 us (2%)
  starting transfers between devices  8.33 us (1%)
    ppermute x5, waiting for transfers between devices, local_fit(): arrived.append(lax.ppermute(piece, 'tp', SWAP))  256 us
    pallas_call x5, Pallas kernels, factor_call(): pl.pallas_call(functools.partial(factor_kernel, first, steps, source, las...  143 us
    dot_general x2, matrix products, gram_of(): lax.dot_general(lhs, rhs, CONTRACT_ROWS, precision=HIGHEST, preferred_ele...  90.3 us
    pallas_call x5, Pallas kernels, cross_call(): pl.pallas_call(cross_kernel, grid_spec=pltpu.PrefetchScalarGridSpec(num_s...  77.3 us
    pallas_call x5, Pallas kernels, scatter_call(): pl.pallas_call(functools.partial(scatter_kernel, n), out_shape=jax.ShapeD...  56.1 us
    reduce_scatter x1, waiting for transfers between devices, scatter(): return lax.psum_scatter(partial, 'dp', scatter_dimension=0, tiled=True)  38.4 us
    dynamic_slice x5, local copies, waits for them, and re-layouts, local_fit(): piece = lax.dynamic_slice(design, (offset, at), (part, width))  19.6 us
  transfers between devices with their start and end apart: 13, of which 7 were waited for; matrix products, arithmetic and copies ran while one was open for 7% of the time, Pallas kernels for 31%

profile of v4, /device:TPU:0, one launch (start us, length us, event | category | flops | bytes accessed | tf_op | source)
XLA Modules:
  0.0 749.9 jit_solution(7938316988671602913)
XLA Ops:
  7.2 59.4 %fusion.3 = f32[512,1024]{1,0:T(8,128)} fusion(f32[8192,1024]{1,0:T(8,128)} %design.3), kind=kOutput, calls=%fused_computation.3 | convolution fusion | flops 51539607552 | bytes 52428800 | tf_op jit(solution)/shard_map/dot_general | solution.py:442
  66.7 38.4 %reduce-scatter.2.cloned.1.call-done = f32[64,1024]{1,0:T(8,128)} async-done(((f32[512,1024]{1,0:T(8,128)}), f32[64,1024]{1,0:T(8,128)}) %reduce-scatter.2.cloned.1.call-update) | async-done | bytes 262160 | tf_op jit(solution)/shard_map/reduce_scatter | solution.py:445
  111.1 30.9 %fusion = f32[512,512]{1,0:T(8,128)S(1)} fusion(f32[8192,1024]{1,0:T(8,128)} %design.3), kind=kOutput, calls=%fused_computation | convolution fusion | flops 25769803776 | bytes 34603008 | tf_op jit(solution)/shard_map/dot_general | solution.py:442
  142.2 12.3 %moment.1 = f32[8,1024]{1,0:T(8,128)S(1)} custom-call(f32[8192,1024]{1,0:T(8,128)} %design.3, f32[64,128]{1,0:T(8,128)S(1)} %bitcast.33), custom_call_target="tpu_custom_call" | custom-call | flops 10000000000 | bytes 33554432 | tf_op jit(solution)/shard_map/moment/pallas_call | solution.py:305
  154.5 60.7 %collective-permute-done.got = f32[4096,256]{1,0:T(8,128)} collective-permute-done((f32[4096,256]{1,0:T(8,128)}, f32[4096,256]{1,0:T(8,128)}, u32[]{:S(2)}, u32[]{:S(2)}) %collective-permute-start) | collective-permute-done | bytes 4194336 | tf_op jit(solution)/shard_map/ppermute | solution.py:455
  215.2 17.2 %shard_map.50 = f32[256,1024]{1,0:T(8,128)S(1)} custom-call(s32[1]{0:T(128)} %bitcast.6.base, f32[4096,256]{1,0:T(8,128)} %collective-permute-done.got, f32[8192,1024]{1,0:T(8,128)} %design.3), custom_call_target="tpu_custom_call" | custom-call | flops 2147483648 | bytes 20971520 | tf_op jit(solution)/shard_map/pallas_call | solution.py:350
  232.7 18.1 %shard_map.51 = f32[72,1024]{1,0:T(8,128)} custom-call(f32[576,1024]{1,0:T(8,128)S(1)} %bitcast.31), custom_call_target="tpu_custom_call" | custom-call | flops 10000000000 | bytes 1179648 | tf_op jit(solution)/shard_map/pallas_call | solution.py:410
  256.9 106.2 %collective-permute-done.1.got = f32[4096,256]{1,0:T(8,128)} collective-permute-done((f32[4096,256]{1,0:T(8,128)}, f32[4096,256]{1,0:T(8,128)}, u32[]{:S(2)}, u32[]{:S(2)}) %collective-permute-start.1) | collective-permute-done | bytes 4194336 | tf_op jit(solution)/shard_map/ppermute | solution.py:455
  363.1 17.4 %shard_map.52.part = f32[256,1024]{1,0:T(8,128)S(1)} custom-call(s32[1]{0:T(128)} %bitcast.6.base, f32[4096,256]{1,0:T(8,128)} %collective-permute-done.1.got, f32[8192,1024]{1,0:T(8,128)} %design.3), custom_call_target="tpu_custom_call" | custom-call | flops 2147483648 | bytes 20971520 | tf_op jit(solution)/shard_map/pallas_call | solution.py:350
  380.5 11.0 %shard_map.53 = f32[32,1024]{1,0:T(8,128)} custom-call(f32[256,1024]{1,0:T(8,128)S(1)} %shard_map.52.part), custom_call_target="tpu_custom_call" | custom-call | flops 10000000000 | bytes 524288 | tf_op jit(solution)/shard_map/pallas_call | solution.py:410
  398.3 20.6 %shard_map.54 = (f32[28,256,256]{2,1,0:T(8,128)}, f32[8,2,256,256]{3,2,1,0:T(8,128)S(1)}, f32[8,8,256]{2,1,0:T(8,128)S(1)}) custom-call(f32[1,1]{1,0:T(1,128)} %bitcast.27.refs_0_, f32[2,512,1024]{2,1,0:T(8,128)} %bitcast.53, f32[2,8,72,1024]{3,2,1,0:T(8,128)} %bitcast.48), custom_call_target="tpu_custom_call" | custom-call | flops 40000000000 | bytes 8388608 | tf_op jit(solution)/shard_map/pallas_call | solution.py:257
  429.6 27.4 %shard_map.55 = (f32[28,256,256]{2,1,0:T(8,128)}, f32[8,2,256,256]{3,2,1,0:T(8,128)}, f32[8,8,256]{2,1,0:T(8,128)S(1)}) custom-call(f32[1,1]{1,0:T(1,128)} %bitcast.25.refs_0_, f32[2,512,1024]{2,1,0:T(8,128)} %bitcast.54, f32[2,8,72,1024]{3,2,1,0:T(8,128)} %bitcast.49, ...), custom_call_target="tpu_custom_call", output_to_operand_aliasing={{0}: (4, {}), {1}: (5, {}), {2}: (6, {})} | custom-call | flops 40000000000 | bytes 8388608 | tf_op jit(solution)/shard_map/pallas_call | solution.py:257
  457.0 38.5 %collective-permute-done.2.got = f32[4096,256]{1,0:T(8,128)} collective-permute-done((f32[4096,256]{1,0:T(8,128)}, f32[4096,256]{1,0:T(8,128)}, u32[]{:S(2)}, u32[]{:S(2)}) %collective-permute-start.2) | collective-permute-done | bytes 4194336 | tf_op jit(solution)/shard_map/ppermute | solution.py:455
  495.6 17.2 %shard_map.56.part = f32[256,1024]{1,0:T(8,128)S(1)} custom-call(s32[1]{0:T(128)} %bitcast.6.base, f32[4096,256]{1,0:T(8,128)} %collective-permute-done.2.got, f32[8192,1024]{1,0:T(8,128)} %design.3), custom_call_target="tpu_custom_call" | custom-call | flops 2147483648 | bytes 20971520 | tf_op jit(solution)/shard_map/pallas_call | solution.py:350
  512.8 10.2 %shard_map.57 = f32[32,1024]{1,0:T(8,128)} custom-call(f32[256,1024]{1,0:T(8,128)S(1)} %shard_map.56.part), custom_call_target="tpu_custom_call" | custom-call | flops 10000000000 | bytes 524288 | tf_op jit(solution)/shard_map/pallas_call | solution.py:410
  531.3 50.3 %collective-permute-done.3.got = f32[4096,128]{1,0:T(8,128)} collective-permute-done((f32[4096,128]{1,0:T(8,128)}, f32[4096,128]{1,0:T(8,128)}, u32[]{:S(2)}, u32[]{:S(2)}) %collective-permute-start.3) | collective-permute-done | bytes 2097184 | tf_op jit(solution)/shard_map/ppermute | solution.py:455
  581.6 13.0 %shard_map.58.part = f32[128,1024]{1,0:T(8,128)S(1)} custom-call(s32[1]{0:T(128)} %bitcast.6.base, f32[4096,128]{1,0:T(8,128)} %collective-permute-done.3.got, f32[8192,1024]{1,0:T(8,128)} %design.3), custom_call_target="tpu_custom_call" | custom-call | flops 1073741824 | bytes 18874368 | tf_op jit(solution)/shard_map/pallas_call | solution.py:350
  594.6 8.2 %shard_map.59 = f32[16,1024]{1,0:T(8,128)} custom-call(f32[128,1024]{1,0:T(8,128)S(1)} %shard_map.58.part), custom_call_target="tpu_custom_call" | custom-call | flops 10000000000 | bytes 262144 | tf_op jit(solution)/shard_map/pallas_call | solution.py:410
  606.1 37.4 %shard_map.60 = (f32[28,256,256]{2,1,0:T(8,128)}, f32[8,2,256,256]{3,2,1,0:T(8,128)}, f32[8,8,256]{2,1,0:T(8,128)S(1)}) custom-call(f32[1,1]{1,0:T(1,128)} %bitcast.28.refs_0_, f32[2,512,1024]{2,1,0:T(8,128)} %bitcast.55, f32[2,8,72,1024]{3,2,1,0:T(8,128)} %bitcast.50, ...), custom_call_target="tpu_custom_call", output_to_operand_aliasing={{0}: (5, {}), {1}: (6, {}), {2}: (7, {})} | custom-call | flops 40000000000 | bytes 8388608 | tf_op jit(solution)/shard_map/pallas_call | solution.py:257
  643.5 12.4 %shard_map.61.part = f32[128,1024]{1,0:T(8,128)S(1)} custom-call(s32[1]{0:T(128)} %bitcast.6.base, f32[4096,128]{1,0:T(8,128)S(1)} %collective-permute-done.4.got, f32[8192,1024]{1,0:T(8,128)} %design.3), custom_call_target="tpu_custom_call" | custom-call | flops 1073741824 | bytes 18874368 | tf_op jit(solution)/shard_map/pallas_call | solution.py:350
  655.8 8.6 %shard_map.62 = f32[16,1024]{1,0:T(8,128)} custom-call(f32[128,1024]{1,0:T(8,128)S(1)} %shard_map.61.part), custom_call_target="tpu_custom_call" | custom-call | flops 10000000000 | bytes 262144 | tf_op jit(solution)/shard_map/pallas_call | solution.py:410
  667.3 25.9 %shard_map.63 = (f32[28,256,256]{2,1,0:T(8,128)}, f32[8,2,256,256]{3,2,1,0:T(8,128)}, f32[8,8,256]{2,1,0:T(8,128)S(1)}) custom-call(f32[1,1]{1,0:T(1,128)} %bitcast.29.refs_0_, f32[2,512,1024]{2,1,0:T(8,128)} %bitcast.56, f32[2,8,72,1024]{3,2,1,0:T(8,128)} %bitcast.51, ...), custom_call_target="tpu_custom_call", output_to_operand_aliasing={{0}: (6, {}), {1}: (7, {}), {2}: (8, {})} | custom-call | flops 20000000000 | bytes 8388608 | tf_op jit(solution)/shard_map/pallas_call | solution.py:257
  694.5 31.3 %shard_map.64 = (f32[28,256,256]{2,1,0:T(8,128)}, f32[8,2,256,256]{3,2,1,0:T(8,128)}, f32[8,8,256]{2,1,0:T(8,128)S(1)}, f32[2,1024]{1,0:T(2,128)S(1)}) custom-call(f32[1,1]{1,0:T(1,128)} %bitcast.26.refs_0_, f32[2,512,1024]{2,1,0:T(8,128)} %bitcast.57, f32[2,8,72,1024]{3,2,1,0:T(8,128)} %bitcast.52, ...), custom_call_target="tpu_custom_call", output_to_operand_aliasing={{0}: (7, {}), {1}: (8, {}), {2}: (9, {})} | custom-call | flops 20000000000 | bytes 8388608 | tf_op jit(solution)/shard_map/pallas_call | solution.py:257
  725.8 12.2 %fit.1 = f32[64,128]{1,0:T(8,128)S(1)} custom-call(f32[8192,1024]{1,0:T(8,128)} %design.3, f32[1,1024]{1,0:T(1,128)S(1)} %constant_dynamic-slice_fusion.4.coeff), custom_call_target="tpu_custom_call" | custom-call | flops 10000000000 | bytes 33554432 | tf_op jit(solution)/shard_map/fit/pallas_call | solution.py:327
  (61 shorter events, 49.4 us)
Async XLA Ops:
  7.2 97.9 %reduce-scatter.2.cloned.1.call-start = ((), (), s32[]{:S(2)}) async-start(), calls=%async_computation.1 | async-start | bytes 2359296 | tf_op jit(solution)/shard_map/reduce_scatter | solution.py:445
  66.6 331.7 %all-gather.7.cloned.1.call-start = ((), (), s32[]{:S(2)}) async-start(), calls=%async_computation.2 | async-start | bytes 4456448 | tf_op jit(solution)/shard_map/all_gather | solution.py:448
  105.1 293.2 %all-gather.9.cloned.1.call-start = ((), (), s32[]{:S(2)}) async-start(), calls=%async_computation.3 | async-start | bytes 5013504 | tf_op jit(solution)/shard_map/all_gather | solution.py:448
  109.6 105.6 %collective-permute-start = (f32[4096,256]{1,0:T(8,128)}, f32[4096,256]{1,0:T(8,128)}, u32[]{:S(2)}, u32[]{:S(2)}) collective-permute-start(f32[4096,256]{1,0:T(8,128)} %constant_dynamic-slice_fusion.5), channel_id=1, source_target_pairs={{0,8},{8,0},{1,9},{9,1},{2,10},{10,2},{3,11},{11,3},{4,12},{12,4},... | collective-permute-start | bytes 12582920 | tf_op jit(solution)/shard_map/ppermute | solution.py:455
  111.1 31.1 %copy-start = (f32[8192]{0:T(1024)S(1)}, f32[8192]{0:T(1024)}, u32[]{:S(2)}) copy-start(f32[8192]{0:T(1024)} %param.4) | copy-start | bytes 98308
  250.9 177.1 %all-gather.11.cloned.1.call-start = ((), (), s32[]{:S(2)}) async-start(), calls=%async_computation.4 | async-start | bytes 2228224 | tf_op jit(solution)/shard_map/all_gather | solution.py:448
  255.4 107.7 %collective-permute-start.1 = (f32[4096,256]{1,0:T(8,128)}, f32[4096,256]{1,0:T(8,128)}, u32[]{:S(2)}, u32[]{:S(2)}) collective-permute-start(f32[4096,256]{1,0:T(8,128)} %constant_dynamic-slice_fusion.3), channel_id=1, source_target_pairs={{0,8},{8,0},{1,9},{9,1},{2,10},{10,2},{3,11},{11,3},{4,12},{12,4},... | collective-permute-start | bytes 12582920 | tf_op jit(solution)/shard_map/ppermute | solution.py:455
  391.5 211.3 %all-gather.13.cloned.1.call-start = ((), (), s32[]{:S(2)}) async-start(), calls=%async_computation.5 | async-start | bytes 2228224 | tf_op jit(solution)/shard_map/all_gather | solution.py:448
  396.1 99.5 %collective-permute-start.2 = (f32[4096,256]{1,0:T(8,128)}, f32[4096,256]{1,0:T(8,128)}, u32[]{:S(2)}, u32[]{:S(2)}) collective-permute-start(f32[4096,256]{1,0:T(8,128)} %constant_dynamic-slice_fusion.2), channel_id=1, source_target_pairs={{0,8},{8,0},{1,9},{9,1},{2,10},{10,2},{3,11},{11,3},{4,12},{12,4},... | collective-permute-start | bytes 12582920 | tf_op jit(solution)/shard_map/ppermute | solution.py:455
  418.9 2.0 copy-start.10
  428.0 1.6 copy-start.2
  523.1 141.4 %all-gather.15.cloned.1.call-start = ((), (), s32[]{:S(2)}) async-start(), calls=%async_computation.6 | async-start | bytes 1114112 | tf_op jit(solution)/shard_map/all_gather | solution.py:448
  526.2 55.4 %collective-permute-start.3 = (f32[4096,128]{1,0:T(8,128)}, f32[4096,128]{1,0:T(8,128)}, u32[]{:S(2)}, u32[]{:S(2)}) collective-permute-start(f32[4096,128]{1,0:T(8,128)} %constant_dynamic-slice_fusion.1), channel_id=1, source_target_pairs={{0,8},{8,0},{1,9},{9,1},{2,10},{10,2},{3,11},{11,3},{4,12},{12,4},... | collective-permute-start | bytes 6291464 | tf_op jit(solution)/shard_map/ppermute | solution.py:455
  530.7 112.7 %collective-permute-start.4 = (f32[4096,128]{1,0:T(8,128)}, f32[4096,128]{1,0:T(8,128)S(1)}, u32[]{:S(2)}, u32[]{:S(2)}) collective-permute-start(f32[4096,128]{1,0:T(8,128)} %constant_dynamic-slice_fusion), channel_id=1, source_target_pairs={{0,8},{8,0},{1,9},{9,1},{2,10},{10,2},{3,11},{11,3},{4,12},{12,4},... | collective-permute-start | bytes 6291464 | tf_op jit(solution)/shard_map/ppermute | solution.py:455
  602.8 90.4 %all-gather.17.cloned.1.call-start = ((), (), s32[]{:S(2)}) async-start(), calls=%async_computation.7 | async-start | bytes 1114112 | tf_op jit(solution)/shard_map/all_gather | solution.py:448
  602.9 1.6 copy-start.3
  604.5 1.6 copy-start.5
  655.8 8.7 %copy-start.4 = (f32[512,1024]{1,0:T(8,128)S(1)}, f32[512,1024]{1,0:T(8,128)}, u32[]{:S(2)}) copy-start(f32[512,1024]{1,0:T(8,128)} %all-gather.11.cloned.1.call-done) | copy-start | bytes 6291460
  664.5 1.6 copy-start.6
  666.1 1.2 copy-start.7
  667.3 25.9 %copy-start.8 = (f32[256,1024]{1,0:T(8,128)S(1)}, f32[256,1024]{1,0:T(8,128)}, u32[]{:S(2)}) copy-start(f32[256,1024]{1,0:T(8,128)} %all-gather.15.cloned.1.call-done) | copy-start | bytes 3145732
  693.3 1.2 copy-start.9
  725.8 16.1 %copy-start.1 = (f32[8192]{0:T(1024)S(1)}, f32[8192]{0:T(1024)}, u32[]{:S(2)}) copy-start(f32[8192]{0:T(1024)} %param.4) | copy-start | bytes 98308
  738.0 4.0 collective-permute-start.5
Sparse Core Ops, SparseCore 0:
  66.8 38.2 reduce-scatter.1
  107.3 48.7 all-gather.6
  251.0 52.0 all-gather.8
  391.7 36.2 all-gather.10
  523.2 36.3 all-gather.12
  602.9 27.8 all-gather.14
  664.6 25.7 all-gather.16

commit v5 on v4

--- a/solution.py
+++ b/solution.py
@@ -12,7 +12,7 @@
 CONTRACT_ROWS = (((0,), (0,)), ((), ()))
 SUB = 128
 BLK = 2 * SUB
-CHUNKS = (256, 256, 256, 128, 128)
+CHUNKS = (256, 256, 128, 128, 128, 128)
 SWAP = ((0, 1), (1, 0))
 MESH = pl.DeviceIdType.MESH
 TILE = 512
@@ -78,10 +78,12 @@
     refs = refs[3 + n_cc :]
     if first:
         refs = refs[3:]
+    if last:
+        side, design_hbm, refs = refs[0][0, 0], refs[1], refs[2:]
     low_hbm, inv_hbm, half_hbm = refs[0], refs[1], refs[2]
     refs = refs[3:]
     if last:
-        x_ref, refs = refs[0], refs[1:]
+        x_ref, fit_ref, whole, whole_sem, refs = refs[0], refs[1], refs[-2], refs[-1], refs[2:-2]
     low, inv, half, diag, cross, prev, mom, panel, work, acc, up, rows, sems, wsems = refs
     end = first + steps
     width = SUB * steps
@@ -126,6 +128,9 @@
     for copy in loads:
         copy.wait()
     lam = ridge[0, 0]
+    if last:
+        fetch = pltpu.make_async_copy(design_hbm, whole, whole_sem)
+        fetch.start()
 
     def step(st, carry):
         k = first + st
@@ -233,9 +238,20 @@
         return carry
 
     lax.fori_loop(0, end, backward, 0)
-
-
-def factor_call(first, steps, source, last, n_blocks, ridge, top, rest, ccs, state):
+    coeff = jnp.where(side == 0, x_ref[0:1, :], x_ref[1:2, :])
+    fetch.wait()
+
+    def fit(i, carry):
+        for q in range(4):
+            at = pl.ds(pl.multiple_of((4 * i + q) * SUB, SUB), SUB)
+            prod = sum(whole[at, g : g + SUB] * coeff[:, g : g + SUB] for g in range(0, whole.shape[1], SUB))
+            fit_ref[pl.ds(4 * i + q, 1), :] = jnp.sum(prod.T, axis=0, keepdims=True)
+        return carry
+
+    lax.fori_loop(0, whole.shape[0] // (4 * SUB), fit, 0)
+
+
+def factor_call(first, steps, source, last, n_blocks, ridge, top, rest, ccs, state, side, design):
     n_low = tri(n_blocks, 0)
     shapes = [
         jax.ShapeDtypeStruct((n_low, BLK, BLK), jnp.float32),
@@ -251,8 +267,14 @@
         in_specs += [hbm] * 3
         args += list(state)
     out_shape, out_specs = list(shapes), [hbm] * 3
+    extra = []
     if last:
+        in_specs += [pl.BlockSpec(memory_space=pltpu.SMEM), hbm]
+        args += [side, design]
         out_shape.append(jax.ShapeDtypeStruct((2, n_blocks * SUB), jnp.float32))
+        out_specs.append(pl.BlockSpec(memory_space=pltpu.VMEM))
+        extra = [pltpu.VMEM(design.shape, jnp.float32), pltpu.SemaphoreType.DMA]
+        out_shape.append(jax.ShapeDtypeStruct((design.shape[0] // SUB, SUB), jnp.float32))
         out_specs.append(pl.BlockSpec(memory_space=pltpu.VMEM))
     res = pl.pallas_call(
         functools.partial(factor_kernel, first, steps, source, last, len(ccs)),
@@ -275,11 +297,12 @@
             pltpu.VMEM((SUB, SUB), jnp.float32),
             pltpu.SemaphoreType.DMA((80,)),
             pltpu.SemaphoreType.DMA((4,)),
+            *extra,
         ],
-        compiler_params=pltpu.CompilerParams(vmem_limit_bytes=48 * 1024 * 1024),
+        compiler_params=pltpu.CompilerParams(vmem_limit_bytes=60 << 20),
         cost_estimate=pl.CostEstimate(flops=int(2e10) * steps, bytes_accessed=8 << 20, transcendentals=0),
     )(*args)
-    return res[:3], (res[3] if last else None)
+    return res[:3], res[3:]
 
 
 def moment_kernel(design, target, out, acc):
@@ -313,27 +336,6 @@
         cost_estimate=pl.CostEstimate(flops=int(1e10), bytes_accessed=4 * rows * cols, transcendentals=0),
         name="moment",
     )(design, target.reshape(rows // SUB, SUB))
-
-
-def fit_kernel(design, coeff, out):
-    i = pl.program_id(0)
-    for q in range(design.shape[0] // SUB):
-        prod = sum(design[SUB * q : SUB * q + SUB, g : g + SUB] * coeff[0:1, g : g + SUB] for g in range(0, design.shape[1], SUB))
-        out[pl.ds(i * (design.shape[0] // SUB) + q, 1), :] = jnp.sum(prod.T, axis=0, keepdims=True)
-
-
-def fit_call(design, coeff):
-    rows, cols = design.shape
-    return pl.pallas_call(
-        fit_kernel,
-        grid=(rows // STREAM,),
-        out_shape=jax.ShapeDtypeStruct((rows // SUB, SUB), jnp.float32),
-        in_specs=[pl.BlockSpec((STREAM, cols), lambda i: (i, 0)), pl.BlockSpec((1, cols), lambda i: (0, 0))],
-        out_specs=pl.BlockSpec((rows // SUB, SUB), lambda i: (0, 0)),
-        compiler_params=pltpu.CompilerParams(vmem_limit_bytes=40 << 20),
-        cost_estimate=pl.CostEstimate(flops=int(1e10), bytes_accessed=4 * rows * cols, transcendentals=0),
-        name="fit",
-    )(design, coeff)
 
 
 def cross_kernel(base, got, kept, out):
@@ -472,33 +474,28 @@
         source = []
         for n, width in enumerate(CHUNKS):
             source += [(n, c) for c in range(0, width, SUB)]
-        lam = ridge.reshape(1, 1)
+        lam, where = ridge.reshape(1, 1), side.astype(jnp.int32).reshape(1, 1)
         ccs, counts = [], [width // SUB for width in CHUNKS]
 
         def factor(n, state, *deps):
             first = sum(counts[:n])
             return factor_call(
                 first, counts[n], tuple(source[: first + counts[n]]), n == len(CHUNKS) - 1, cols // SUB,
-                after(lam, *deps), top, rest, ccs[:n], state,
+                after(lam, *deps), top, rest, ccs[:n], state, where, design,
             )
 
-        rs1 = scatter_call(groups, 1, cross(1, rest_rs))
-        rest = gather(rest_rs).reshape(2, groups, -1, cols)
-        ccs.append(gather(rs1))
-        state, _ = factor(0, None, rs1)
-        state, _ = factor(1, state)
-        rs2 = scatter_call(groups, 2, cross(2, *state))
-        ccs.append(gather(rs2))
-        rs3 = scatter_call(groups, 3, cross(3, rs2))
-        ccs.append(gather(rs3))
-        state, _ = factor(2, state, rs3)
-        rs4 = scatter_call(groups, 4, cross(4, *state))
-        ccs.append(gather(rs4))
-        state, _ = factor(3, state, rs4)
-        _, coeff = factor(4, state)
-
-        mine = lax.dynamic_slice_in_dim(coeff, side, 1)
-        fit = fit_call(design, mine)
+        state, coeff, summed = None, None, rest_rs
+        for n in range(1, len(CHUNKS) + 1):
+            if n < len(CHUNKS):
+                summed = scatter_call(groups, n, cross(n, summed, *(state or ())))
+            if n == 1:
+                rest = gather(rest_rs).reshape(2, groups, -1, cols)
+            if n < len(CHUNKS):
+                fresh = gather(summed)
+            state, coeff = factor(n - 1, state, summed)
+            ccs.append(fresh)
+
+        coeff, fit = coeff
         fitted = fit + lax.ppermute(fit, "tp", SWAP)
         return coeff.reshape(2 * cols), target - fitted.reshape(rows)
 

time: 760 us -> 665 us (0.88)
  waiting for transfers between devices: 303 us -> 209 us
  local copies, waits for them, and re-layouts: 31 us -> 22.7 us
    ppermute x5 -> x6, waiting for transfers between devices: 256 us -> 167 us  [local_fit(): arrived.append(lax.ppermute(piece, 'tp', SWAP))]
    pallas_call x1 -> x0, Pallas kernels: 12.2 us -> none  [fit_call(): pl.pallas_call(fit_kernel, grid=(rows // STREAM,), out_shape=jax.ShapeDty...]
    unnamed x23 -> x5, local copies, waits for them, and re-layouts: 11.4 us -> 1.3 us
    pallas_call x5 -> x6, Pallas kernels: 143 us -> 152 us  [factor_call(): pl.pallas_call(functools.partial(factor_kernel, first, steps, source, las...]
    pallas_call x5 -> x6, Pallas kernels: 77.3 us -> 85.7 us  [cross_call(): pl.pallas_call(cross_kernel, grid_spec=pltpu.PrefetchScalarGridSpec(num_s...]
    dynamic_slice x5 -> x6, local copies, waits for them, and re-layouts: 19.6 us -> 21.3 us  [local_fit(): piece = lax.dynamic_slice(design, (offset, at), (part, width))]
    pallas_call x5 -> x6, Pallas kernels: 56.1 us -> 57.1 us  [scatter_call(): pl.pallas_call(functools.partial(scatter_kernel, n), out_shape=jax.ShapeD...]
  transfers between devices with their start and end apart: 13 -> 15, of which waited for: 7 -> 8; matrix products, arithmetic and copies ran while one was open for 7% -> 8% of each run, Pallas kernels for 31% -> 42%
where the time goes in v5:
time: 665 us; the launch traced here: 655 us
  Pallas kernels  307 us (46%)
  waiting for transfers between devices  209 us (31%)
  matrix products  90.3 us (14%)
  local copies, waits for them, and re-layouts  22.7 us (3%)
  between operations  15.2 us (2%)
  starting transfers between devices  8.76 us (1%)
    ppermute x6, waiting for transfers between devices, local_fit(): arrived.append(lax.ppermute(piece, 'tp', SWAP))  167 us
    pallas_call x6, Pallas kernels, factor_call(): pl.pallas_call(functools.partial(factor_kernel, first, steps, source, las...  152 us
    dot_general x2, matrix products, gram_of(): lax.dot_general(lhs, rhs, CONTRACT_ROWS, precision=HIGHEST, preferred_ele...  90.3 us
    pallas_call x6, Pallas kernels, cross_call(): pl.pallas_call(cross_kernel, grid_spec=pltpu.PrefetchScalarGridSpec(num_s...  85.7 us
    pallas_call x6, Pallas kernels, scatter_call(): pl.pallas_call(functools.partial(scatter_kernel, n), out_shape=jax.ShapeD...  57.1 us
    reduce_scatter x1, waiting for transfers between devices, scatter(): return lax.psum_scatter(partial, 'dp', scatter_dimension=0, tiled=True)  38.4 us
    dynamic_slice x6, local copies, waits for them, and re-layouts, local_fit(): piece = lax.dynamic_slice(design, (offset, at), (part, width))  21.3 us
  transfers between devices with their start and end apart: 15, of which 8 were waited for; matrix products, arithmetic and copies ran while one was open for 8% of the time, Pallas kernels for 42%

profile of v5, /device:TPU:0, one launch (start us, length us, event | category | flops | bytes accessed | tf_op | source)
XLA Modules:
  0.0 654.5 jit_solution(2908474353965983204)
XLA Ops:
  7.2 59.4 %fusion.3 = f32[512,1024]{1,0:T(8,128)} fusion(f32[8192,1024]{1,0:T(8,128)} %refs_12_.1), kind=kOutput, calls=%fused_computation.3 | convolution fusion | flops 51539607552 | bytes 52428800 | tf_op jit(solution)/shard_map/dot_general | solution.py:444
  66.7 38.4 %reduce-scatter.2.cloned.1.call-done = f32[64,1024]{1,0:T(8,128)} async-done(((f32[512,1024]{1,0:T(8,128)}), f32[64,1024]{1,0:T(8,128)}) %reduce-scatter.2.cloned.1.call-update) | async-done | bytes 262160 | tf_op jit(solution)/shard_map/reduce_scatter | solution.py:447
  111.1 30.9 %fusion = f32[512,512]{1,0:T(8,128)S(1)} fusion(f32[8192,1024]{1,0:T(8,128)} %refs_12_.1), kind=kOutput, calls=%fused_computation | convolution fusion | flops 25769803776 | bytes 34603008 | tf_op jit(solution)/shard_map/dot_general | solution.py:444
  142.1 12.3 %moment.1 = f32[8,1024]{1,0:T(8,128)S(1)} custom-call(f32[8192,1024]{1,0:T(8,128)} %refs_12_.1, f32[64,128]{1,0:T(8,128)S(1)} %bitcast.36), custom_call_target="tpu_custom_call" | custom-call | flops 10000000000 | bytes 33554432 | tf_op jit(solution)/shard_map/moment/pallas_call | solution.py:328
  154.5 60.7 %collective-permute-done.got = f32[4096,256]{1,0:T(8,128)} collective-permute-done((f32[4096,256]{1,0:T(8,128)}, f32[4096,256]{1,0:T(8,128)}, u32[]{:S(2)}, u32[]{:S(2)}) %collective-permute-start) | collective-permute-done | bytes 4194336 | tf_op jit(solution)/shard_map/ppermute | solution.py:457
  215.2 17.2 %shard_map.50 = f32[256,1024]{1,0:T(8,128)S(1)} custom-call(s32[1]{0:T(128)} %bitcast.1.base, f32[4096,256]{1,0:T(8,128)} %collective-permute-done.got, f32[8192,1024]{1,0:T(8,128)} %refs_12_.1), custom_call_target="tpu_custom_call" | custom-call | flops 2147483648 | bytes 20971520 | tf_op jit(solution)/shard_map/pallas_call | solution.py:352
  232.7 18.1 %shard_map.51 = f32[72,1024]{1,0:T(8,128)} custom-call(f32[576,1024]{1,0:T(8,128)S(1)} %bitcast.34), custom_call_target="tpu_custom_call" | custom-call | flops 10000000000 | bytes 1179648 | tf_op jit(solution)/shard_map/pallas_call | solution.py:412
  274.0 89.9 %collective-permute-done.1.got = f32[4096,256]{1,0:T(8,128)} collective-permute-done((f32[4096,256]{1,0:T(8,128)}, f32[4096,256]{1,0:T(8,128)}, u32[]{:S(2)}, u32[]{:S(2)}) %collective-permute-start.1) | collective-permute-done | bytes 4194336 | tf_op jit(solution)/shard_map/ppermute | solution.py:457
  363.9 17.6 %shard_map.52.part = f32[256,1024]{1,0:T(8,128)S(1)} custom-call(s32[1]{0:T(128)} %bitcast.1.base, f32[4096,256]{1,0:T(8,128)} %collective-permute-done.1.got, f32[8192,1024]{1,0:T(8,128)} %refs_12_.1), custom_call_target="tpu_custom_call" | custom-call | flops 2147483648 | bytes 20971520 | tf_op jit(solution)/shard_map/pallas_call | solution.py:352
  381.5 9.7 %shard_map.53 = f32[32,1024]{1,0:T(8,128)} custom-call(f32[256,1024]{1,0:T(8,128)S(1)} %shard_map.52.part), custom_call_target="tpu_custom_call" | custom-call | flops 10000000000 | bytes 524288 | tf_op jit(solution)/shard_map/pallas_call | solution.py:412
  391.3 20.7 %shard_map.54 = (f32[28,256,256]{2,1,0:T(8,128)}, f32[8,2,256,256]{3,2,1,0:T(8,128)}, f32[8,8,256]{2,1,0:T(8,128)}) custom-call(f32[1,1]{1,0:T(1,128)} %bitcast.27.refs_0_, f32[2,512,1024]{2,1,0:T(8,128)} %bitcast.47, f32[2,8,72,1024]{3,2,1,0:T(8,128)} %bitcast.41), custom_call_target="tpu_custom_call" | custom-call | flops 40000000000 | bytes 8388608 | tf_op jit(solution)/shard_map/pallas_call | solution.py:279
  412.1 13.0 %shard_map.55.part = f32[128,1024]{1,0:T(8,128)S(1)} custom-call(s32[1]{0:T(128)} %bitcast.1.base, f32[4096,128]{1,0:T(8,128)} %collective-permute-done.2.got, f32[8192,1024]{1,0:T(8,128)} %refs_12_.1), custom_call_target="tpu_custom_call" | custom-call | flops 1073741824 | bytes 18874368 | tf_op jit(solution)/shard_map/pallas_call | solution.py:352
  425.0 9.2 %shard_map.56 = f32[16,1024]{1,0:T(8,128)} custom-call(f32[128,1024]{1,0:T(8,128)S(1)} %shard_map.55.part), custom_call_target="tpu_custom_call" | custom-call | flops 10000000000 | bytes 262144 | tf_op jit(solution)/shard_map/pallas_call | solution.py:412
  434.3 27.8 %shard_map.57 = (f32[28,256,256]{2,1,0:T(8,128)}, f32[8,2,256,256]{3,2,1,0:T(8,128)}, f32[8,8,256]{2,1,0:T(8,128)}) custom-call(f32[1,1]{1,0:T(1,128)} %bitcast.28.refs_0_, f32[2,512,1024]{2,1,0:T(8,128)} %bitcast.48, f32[2,8,72,1024]{3,2,1,0:T(8,128)} %bitcast.42, ...), custom_call_target="tpu_custom_call", output_to_operand_aliasing={{0}: (4, {}), {1}: (5, {}), {2}: (6, {})} | custom-call | flops 40000000000 | bytes 8388608 | tf_op jit(solution)/shard_map/pallas_call | solution.py:279
  463.6 12.3 %shard_map.58.part = f32[128,1024]{1,0:T(8,128)S(1)} custom-call(s32[1]{0:T(128)} %bitcast.1.base, f32[4096,128]{1,0:T(8,128)S(1)} %collective-permute-done.3.got, f32[8192,1024]{1,0:T(8,128)} %refs_12_.1), custom_call_target="tpu_custom_call" | custom-call | flops 1073741824 | bytes 18874368 | tf_op jit(solution)/shard_map/pallas_call | solution.py:352
  475.9 6.9 %shard_map.59 = f32[16,1024]{1,0:T(8,128)} custom-call(f32[128,1024]{1,0:T(8,128)S(1)} %shard_map.58.part), custom_call_target="tpu_custom_call" | custom-call | flops 10000000000 | bytes 262144 | tf_op jit(solution)/shard_map/pallas_call | solution.py:412
  482.9 19.4 %shard_map.60 = (f32[28,256,256]{2,1,0:T(8,128)}, f32[8,2,256,256]{3,2,1,0:T(8,128)}, f32[8,8,256]{2,1,0:T(8,128)}) custom-call(f32[1,1]{1,0:T(1,128)} %bitcast.29.refs_0_, f32[2,512,1024]{2,1,0:T(8,128)} %bitcast.49, f32[2,8,72,1024]{3,2,1,0:T(8,128)} %bitcast.43, ...), custom_call_target="tpu_custom_call", output_to_operand_aliasing={{0}: (5, {}), {1}: (6, {}), {2}: (7, {})} | custom-call | flops 20000000000 | bytes 8388608 | tf_op jit(solution)/shard_map/pallas_call | solution.py:279
  502.3 9.6 %collective-permute-done.4.got = f32[4096,128]{1,0:T(8,128)} collective-permute-done((f32[4096,128]{1,0:T(8,128)}, f32[4096,128]{1,0:T(8,128)}, u32[]{:S(2)}, u32[]{:S(2)}) %collective-permute-start.4) | collective-permute-done | bytes 2097184 | tf_op jit(solution)/shard_map/ppermute | solution.py:457
  511.9 12.8 %shard_map.61.part = f32[128,1024]{1,0:T(8,128)S(1)} custom-call(s32[1]{0:T(128)} %bitcast.1.base, f32[4096,128]{1,0:T(8,128)} %collective-permute-done.4.got, f32[8192,1024]{1,0:T(8,128)} %refs_12_.1), custom_call_target="tpu_custom_call" | custom-call | flops 1073741824 | bytes 18874368 | tf_op jit(solution)/shard_map/pallas_call | solution.py:352
  531.4 22.5 %shard_map.63 = (f32[28,256,256]{2,1,0:T(8,128)}, f32[8,2,256,256]{3,2,1,0:T(8,128)}, f32[8,8,256]{2,1,0:T(8,128)}) custom-call(f32[1,1]{1,0:T(1,128)} %bitcast.30.refs_0_, f32[2,512,1024]{2,1,0:T(8,128)} %bitcast.50, f32[2,8,72,1024]{3,2,1,0:T(8,128)} %bitcast.44, ...), custom_call_target="tpu_custom_call", output_to_operand_aliasing={{0}: (6, {}), {1}: (7, {}), {2}: (8, {})} | custom-call | flops 20000000000 | bytes 8388608 | tf_op jit(solution)/shard_map/pallas_call | solution.py:279
  559.3 12.8 %shard_map.64.part = f32[128,1024]{1,0:T(8,128)S(1)} custom-call(s32[1]{0:T(128)} %bitcast.1.base, f32[4096,128]{1,0:T(8,128)} %collective-permute-done.5.got, f32[8192,1024]{1,0:T(8,128)} %refs_12_.1), custom_call_target="tpu_custom_call" | custom-call | flops 1073741824 | bytes 18874368 | tf_op jit(solution)/shard_map/pallas_call | solution.py:352
  572.1 6.6 %shard_map.65 = f32[16,1024]{1,0:T(8,128)} custom-call(f32[128,1024]{1,0:T(8,128)S(1)} %shard_map.64.part), custom_call_target="tpu_custom_call" | custom-call | flops 10000000000 | bytes 262144 | tf_op jit(solution)/shard_map/pallas_call | solution.py:412
  578.8 26.2 %shard_map.66 = (f32[28,256,256]{2,1,0:T(8,128)}, f32[8,2,256,256]{3,2,1,0:T(8,128)}, f32[8,8,256]{2,1,0:T(8,128)}) custom-call(f32[1,1]{1,0:T(1,128)} %bitcast.31.refs_0_, f32[2,512,1024]{2,1,0:T(8,128)} %bitcast.51, f32[2,8,72,1024]{3,2,1,0:T(8,128)} %bitcast.45, ...), custom_call_target="tpu_custom_call", output_to_operand_aliasing={{0}: (7, {}), {1}: (8, {}), {2}: (9, {})} | custom-call | flops 20000000000 | bytes 8388608 | tf_op jit(solution)/shard_map/pallas_call | solution.py:279
  606.3 35.7 %shard_map.67 = (f32[28,256,256]{2,1,0:T(8,128)}, f32[8,2,256,256]{3,2,1,0:T(8,128)}, f32[8,8,256]{2,1,0:T(8,128)}, f32[2,1024]{1,0:T(2,128)}, f32[64,128]{1,0:T(8,128)}) custom-call(f32[1,1]{1,0:T(1,128)} %bitcast.32.refs_0_, f32[2,512,1024]{2,1,0:T(8,128)} %bitcast.52, ...), custom_call_target="tpu_custom_call", output_to_operand_aliasing={{0}: (8, {}), {1}: (9, {}), {2}: (10, {})} | custom-call | flops 20000000000 | bytes 8388608 | tf_op jit(solution)/shard_map/pallas_call | solution.py:279
  (50 shorter events, 49.6 us)
Async XLA Ops:
  7.2 97.9 %reduce-scatter.2.cloned.1.call-start = ((), (), s32[]{:S(2)}) async-start(), calls=%async_computation.1 | async-start | bytes 2359296 | tf_op jit(solution)/shard_map/reduce_scatter | solution.py:447
  66.6 324.7 %all-gather.8.cloned.1.call-start = ((), (), s32[]{:S(2)}) async-start(), calls=%async_computation.2 | async-start | bytes 4456448 | tf_op jit(solution)/shard_map/all_gather | solution.py:450
  105.1 286.2 %all-gather.10.cloned.1.call-start = ((), (), s32[]{:S(2)}) async-start(), calls=%async_computation.3 | async-start | bytes 5013504 | tf_op jit(solution)/shard_map/all_gather | solution.py:450
  109.6 105.6 %collective-permute-start = (f32[4096,256]{1,0:T(8,128)}, f32[4096,256]{1,0:T(8,128)}, u32[]{:S(2)}, u32[]{:S(2)}) collective-permute-start(f32[4096,256]{1,0:T(8,128)} %constant_dynamic-slice_fusion.5), channel_id=1, source_target_pairs={{0,8},{8,0},{1,9},{9,1},{2,10},{10,2},{3,11},{11,3},{4,12},{12,4},... | collective-permute-start | bytes 12582920 | tf_op jit(solution)/shard_map/ppermute | solution.py:457
  111.1 31.1 %copy-start = (f32[8192]{0:T(1024)S(1)}, f32[8192]{0:T(1024)}, u32[]{:S(2)}) copy-start(f32[8192]{0:T(1024)} %param.4) | copy-start | bytes 98308
  250.8 183.5 %all-gather.12.cloned.1.call-start = ((), (), s32[]{:S(2)}) async-start(), calls=%async_computation.4 | async-start | bytes 2228224 | tf_op jit(solution)/shard_map/all_gather | solution.py:450
  255.4 108.5 %collective-permute-start.1 = (f32[4096,256]{1,0:T(8,128)}, f32[4096,256]{1,0:T(8,128)}, u32[]{:S(2)}, u32[]{:S(2)}) collective-permute-start(f32[4096,256]{1,0:T(8,128)} %constant_dynamic-slice_fusion.4), channel_id=1, source_target_pairs={{0,8},{8,0},{1,9},{9,1},{2,10},{10,2},{3,11},{11,3},{4,12},{12,4},... | collective-permute-start | bytes 12582920 | tf_op jit(solution)/shard_map/ppermute | solution.py:457
  260.1 152.0 %collective-permute-start.2 = (f32[4096,128]{1,0:T(8,128)}, f32[4096,128]{1,0:T(8,128)}, u32[]{:S(2)}, u32[]{:S(2)}) collective-permute-start(f32[4096,128]{1,0:T(8,128)} %constant_dynamic-slice_fusion.3), channel_id=1, source_target_pairs={{0,8},{8,0},{1,9},{9,1},{2,10},{10,2},{3,11},{11,3},{4,12},{12,4},... | collective-permute-start | bytes 6291464 | tf_op jit(solution)/shard_map/ppermute | solution.py:457
  263.7 199.9 %collective-permute-start.3 = (f32[4096,128]{1,0:T(8,128)}, f32[4096,128]{1,0:T(8,128)S(1)}, u32[]{:S(2)}, u32[]{:S(2)}) collective-permute-start(f32[4096,128]{1,0:T(8,128)} %constant_dynamic-slice_fusion.2), channel_id=1, source_target_pairs={{0,8},{8,0},{1,9},{9,1},{2,10},{10,2},{3,11},{11,3},{4,12},{12,4},... | collective-permute-start | bytes 6291464 | tf_op jit(solution)/shard_map/ppermute | solution.py:457
  268.2 243.7 %collective-permute-start.4 = (f32[4096,128]{1,0:T(8,128)}, f32[4096,128]{1,0:T(8,128)}, u32[]{:S(2)}, u32[]{:S(2)}) collective-permute-start(f32[4096,128]{1,0:T(8,128)} %constant_dynamic-slice_fusion.1), channel_id=1, source_target_pairs={{0,8},{8,0},{1,9},{9,1},{2,10},{10,2},{3,11},{11,3},{4,12},{12,4},... | collective-permute-start | bytes 6291464 | tf_op jit(solution)/shard_map/ppermute | solution.py:457
  271.8 287.5 %collective-permute-start.5 = (f32[4096,128]{1,0:T(8,128)}, f32[4096,128]{1,0:T(8,128)}, u32[]{:S(2)}, u32[]{:S(2)}) collective-permute-start(f32[4096,128]{1,0:T(8,128)} %constant_dynamic-slice_fusion), channel_id=1, source_target_pairs={{0,8},{8,0},{1,9},{9,1},{2,10},{10,2},{3,11},{11,3},{4,12},{12,4},... | collective-permute-start | bytes 6291464 | tf_op jit(solution)/shard_map/ppermute | solution.py:457
  391.2 91.7 %all-gather.14.cloned.1.call-start = ((), (), s32[]{:S(2)}) async-start(), calls=%async_computation.5 | async-start | bytes 1114112 | tf_op jit(solution)/shard_map/all_gather | solution.py:450
  434.2 97.1 %all-gather.16.cloned.1.call-start = ((), (), s32[]{:S(2)}) async-start(), calls=%async_computation.6 | async-start | bytes 1114112 | tf_op jit(solution)/shard_map/all_gather | solution.py:450
  482.8 95.9 %all-gather.18.cloned.1.call-start = ((), (), s32[]{:S(2)}) async-start(), calls=%async_computation.7 | async-start | bytes 1114112 | tf_op jit(solution)/shard_map/all_gather | solution.py:450
  531.3 75.0 %all-gather.20.cloned.1.call-start = ((), (), s32[]{:S(2)}) async-start(), calls=%async_computation.8 | async-start | bytes 1114112 | tf_op jit(solution)/shard_map/all_gather | solution.py:450
  606.3 39.8 %copy-start.1 = (f32[8192]{0:T(1024)S(1)}, f32[8192]{0:T(1024)}, u32[]{:S(2)}) copy-start(f32[8192]{0:T(1024)} %param.4) | copy-start | bytes 98308
  642.0 4.2 collective-permute-start.6
Sparse Core Ops, SparseCore 0:
  66.7 38.2 reduce-scatter.1
  107.3 48.7 all-gather.7
  251.0 52.0 all-gather.9
  391.4 36.7 all-gather.11
  434.4 29.6 all-gather.13
  482.9 29.9 all-gather.15
  531.4 29.2 all-gather.17
  578.9 27.3 all-gather.19

commit v6 on v5

--- a/solution.py
+++ b/solution.py
@@ -343,7 +343,14 @@
     def _():
         out[...] = jnp.zeros_like(out)
 
-    out[...] += lax.dot_general(got[...], kept[...], CONTRACT_ROWS, precision=HIGHEST, preferred_element_type=jnp.float32)
+    span = kept.shape[1] * SUB // got.shape[1]
+
+    def tile(n, carry):
+        at = pl.ds(pl.multiple_of(n * span, SUB), span)
+        out[:, at] += lax.dot_general(got[...], kept[:, at], CONTRACT_ROWS, precision=HIGHEST, preferred_element_type=jnp.float32)
+        return carry
+
+    lax.fori_loop(0, kept.shape[1] // span, tile, 0)
 
 
 def cross_call(base, got, design):
@@ -361,6 +368,33 @@
         compiler_params=pltpu.CompilerParams(vmem_limit_bytes=40 << 20),
         cost_estimate=pl.CostEstimate(flops=2 * rows * width * cols, bytes_accessed=4 * rows * (cols + width), transcendentals=0),
     )(base, got, design)
+
+
+def gram_kernel(left, right, out):
+    @pl.when(pl.program_id(0) == 0)
+    def _():
+        out[...] = jnp.zeros_like(out)
+
+    def tile(n, carry):
+        at = pl.ds(pl.multiple_of(n * TILE, TILE), TILE)
+        out[:, at] += lax.dot_general(left[...], right[:, at], CONTRACT_ROWS, precision=HIGHEST, preferred_element_type=jnp.float32)
+        return carry
+
+    lax.fori_loop(0, out.shape[1] // TILE, tile, 0)
+
+
+def gram_call(design, half, wide, *deps):
+    rows, cols = design.shape
+    left, right = pl.BlockSpec((TILE, cols // 2), lambda i: (i, half)), pl.BlockSpec((TILE, wide), lambda i: (i, half))
+    return pl.pallas_call(
+        gram_kernel,
+        grid=(rows // TILE,),
+        out_shape=jax.ShapeDtypeStruct((cols // 2, wide), jnp.float32),
+        in_specs=[left, right],
+        out_specs=pl.BlockSpec((cols // 2, wide), lambda i: (0, 0)),
+        compiler_params=pltpu.CompilerParams(vmem_limit_bytes=60 << 20),
+        cost_estimate=pl.CostEstimate(flops=rows * cols * wide, bytes_accessed=8 * rows * cols, transcendentals=0),
+    )(design, after(design, *deps))
 
 
 def scatter_kernel(n, part, out, near, sums, got, near_send, near_recv, send, recv):
@@ -440,9 +474,6 @@
         part = rows // 2
         side = lax.axis_index("tp")
 
-        def gram_of(lhs, rhs):
-            return lax.dot_general(lhs, rhs, CONTRACT_ROWS, precision=HIGHEST, preferred_element_type=jnp.float32)
-
         def scatter(partial):
             return lax.psum_scatter(partial, "dp", scatter_dimension=0, tiled=True)
 
@@ -457,9 +488,9 @@
             arrived.append(lax.ppermute(piece, "tp", SWAP))
         base = ((1 - side) * (part // TILE)).astype(jnp.int32).reshape(1)
 
-        top = gram_of(design[:, : cols // 2], design)
+        top = gram_call(design, 0, cols)
         top_rs = scatter(top)
-        rest = gram_of(after(design, top)[:, cols // 2 :], design[:, cols // 2 :])
+        rest = gram_call(design, 1, cols // 2, top)
         moment = moment_call(design, after(target, rest, top_rs))
         top = gather(top_rs)
         rest = rest.reshape(groups, 2, PACK, cols // 2).swapaxes(1, 2).reshape(groups, PACK, cols)

time: 665 us -> 661 us (level); the launches traced: 655 us -> 660 us
  Pallas kernels: 307 us -> 408 us
  matrix products: 90.3 us -> 0 us
  waiting for transfers between devices: 209 us -> 202 us
    pallas_call x0 -> x2, Pallas kernels: none -> 95.3 us  [gram_call(): pl.pallas_call(gram_kernel, grid=(rows // TILE,), out_shape=jax.ShapeDtyp...]
    dot_general x2 -> x0, matrix products: 90.3 us -> none  [gram_of(): lax.dot_general(lhs, rhs, CONTRACT_ROWS, precision=HIGHEST, preferred_ele...]
  transfers between devices with their start and end apart: 15 -> 15, of which waited for: 8 -> 7; matrix products, arithmetic and copies ran while one was open for 8% -> 4% of each run, Pallas kernels for 42% -> 47%
where the time goes in v6:
time: 661 us; the launch traced here: 660 us
  Pallas kernels  408 us (62%)
  waiting for transfers between devices  202 us (31%)
  local copies, waits for them, and re-layouts  24 us (4%)
  between operations  15.1 us (2%)
  starting transfers between devices  9.11 us (1%)
    ppermute x6, waiting for transfers between devices, local_fit(): arrived.append(lax.ppermute(piece, 'tp', SWAP))  161 us
    pallas_call x6, Pallas kernels, factor_call(): pl.pallas_call(functools.partial(factor_kernel, first, steps, source, las...  152 us
    pallas_call x2, Pallas kernels, gram_call(): pl.pallas_call(gram_kernel, grid=(rows // TILE,), out_shape=jax.ShapeDtyp...  95.3 us
    pallas_call x6, Pallas kernels, cross_call(): pl.pallas_call(cross_kernel, grid_spec=pltpu.PrefetchScalarGridSpec(num_s...  88.9 us
    pallas_call x6, Pallas kernels, scatter_call(): pl.pallas_call(functools.partial(scatter_kernel, n), out_shape=jax.ShapeD...  59.7 us
    reduce_scatter x1, waiting for transfers between devices, scatter(): return lax.psum_scatter(partial, 'dp', scatter_dimension=0, tiled=True)  38.4 us
    dynamic_slice x6, local copies, waits for them, and re-layouts, local_fit(): piece = lax.dynamic_slice(design, (offset, at), (part, width))  21.3 us
  transfers between devices with their start and end apart: 15, of which 7 were waited for; matrix products, arithmetic and copies ran while one was open for 4% of the time, Pallas kernels for 47%

profile of v6, /device:TPU:0, one launch (start us, length us, event | category | flops | bytes accessed | tf_op | source)
XLA Modules:
  0.0 659.9 jit_solution(3670768500804937746)
XLA Ops:
  7.2 62.8 %shard_map.50 = f32[512,1024]{1,0:T(8,128)} custom-call(f32[8192,1024]{1,0:T(8,128)} %refs_12_.1, f32[8192,1024]{1,0:T(8,128)} %refs_12_.1), custom_call_target="tpu_custom_call" | custom-call | flops 8589934592 | bytes 67108864 | tf_op jit(solution)/shard_map/pallas_call | solution.py:389
  70.1 38.4 %reduce-scatter.2.cloned.1.call-done = f32[64,1024]{1,0:T(8,128)} async-done(((f32[512,1024]{1,0:T(8,128)}), f32[64,1024]{1,0:T(8,128)}) %reduce-scatter.2.cloned.1.call-update) | async-done | bytes 262160 | tf_op jit(solution)/shard_map/reduce_scatter | solution.py:478
  114.5 32.5 %shard_map.51 = f32[512,512]{1,0:T(8,128)} custom-call(f32[8192,1024]{1,0:T(8,128)} %refs_12_.1, f32[8192,1024]{1,0:T(8,128)} %refs_12_.1), custom_call_target="tpu_custom_call" | custom-call | flops 4294967296 | bytes 67108864 | tf_op jit(solution)/shard_map/pallas_call | solution.py:389
  148.4 12.3 %moment.1 = f32[8,1024]{1,0:T(8,128)S(1)} custom-call(f32[8192,1024]{1,0:T(8,128)} %refs_12_.1, f32[64,128]{1,0:T(8,128)S(1)} %bitcast.34), custom_call_target="tpu_custom_call" | custom-call | flops 10000000000 | bytes 33554432 | tf_op jit(solution)/shard_map/moment/pallas_call | solution.py:328
  160.7 57.9 %collective-permute-done.got = f32[4096,256]{1,0:T(8,128)} collective-permute-done((f32[4096,256]{1,0:T(8,128)}, f32[4096,256]{1,0:T(8,128)}, u32[]{:S(2)}, u32[]{:S(2)}) %collective-permute-start) | collective-permute-done | bytes 4194336 | tf_op jit(solution)/shard_map/ppermute | solution.py:488
  218.6 19.0 %shard_map.52 = f32[256,1024]{1,0:T(8,128)S(1)} custom-call(s32[1]{0:T(128)} %bitcast.1.base, f32[4096,256]{1,0:T(8,128)} %collective-permute-done.got, f32[8192,1024]{1,0:T(8,128)} %refs_12_.1), custom_call_target="tpu_custom_call" | custom-call | flops 2147483648 | bytes 20971520 | tf_op jit(solution)/shard_map/pallas_call | solution.py:359
  237.9 18.1 %shard_map.53 = f32[72,1024]{1,0:T(8,128)} custom-call(f32[576,1024]{1,0:T(8,128)S(1)} %bitcast.32), custom_call_target="tpu_custom_call" | custom-call | flops 10000000000 | bytes 1179648 | tf_op jit(solution)/shard_map/pallas_call | solution.py:446
  279.2 89.9 %collective-permute-done.1.got = f32[4096,256]{1,0:T(8,128)} collective-permute-done((f32[4096,256]{1,0:T(8,128)}, f32[4096,256]{1,0:T(8,128)}, u32[]{:S(2)}, u32[]{:S(2)}) %collective-permute-start.1) | collective-permute-done | bytes 4194336 | tf_op jit(solution)/shard_map/ppermute | solution.py:488
  369.1 19.0 %shard_map.54.part = f32[256,1024]{1,0:T(8,128)S(1)} custom-call(s32[1]{0:T(128)} %bitcast.1.base, f32[4096,256]{1,0:T(8,128)} %collective-permute-done.1.got, f32[8192,1024]{1,0:T(8,128)} %refs_12_.1), custom_call_target="tpu_custom_call" | custom-call | flops 2147483648 | bytes 20971520 | tf_op jit(solution)/shard_map/pallas_call | solution.py:359
  388.1 9.7 %shard_map.55 = f32[32,1024]{1,0:T(8,128)} custom-call(f32[256,1024]{1,0:T(8,128)S(1)} %shard_map.54.part), custom_call_target="tpu_custom_call" | custom-call | flops 10000000000 | bytes 524288 | tf_op jit(solution)/shard_map/pallas_call | solution.py:446
  398.1 20.7 %shard_map.56 = (f32[28,256,256]{2,1,0:T(8,128)}, f32[8,2,256,256]{3,2,1,0:T(8,128)}, f32[8,8,256]{2,1,0:T(8,128)}) custom-call(f32[1,1]{1,0:T(1,128)} %bitcast.25.refs_0_, f32[2,512,1024]{2,1,0:T(8,128)} %bitcast.45, f32[2,8,72,1024]{3,2,1,0:T(8,128)} %bitcast.39), custom_call_target="tpu_custom_call" | custom-call | flops 40000000000 | bytes 8388608 | tf_op jit(solution)/shard_map/pallas_call | solution.py:279
  418.8 12.9 %shard_map.57.part = f32[128,1024]{1,0:T(8,128)S(1)} custom-call(s32[1]{0:T(128)} %bitcast.1.base, f32[4096,128]{1,0:T(8,128)} %collective-permute-done.2.got, f32[8192,1024]{1,0:T(8,128)} %refs_12_.1), custom_call_target="tpu_custom_call" | custom-call | flops 1073741824 | bytes 18874368 | tf_op jit(solution)/shard_map/pallas_call | solution.py:359
  431.7 9.1 %shard_map.58 = f32[16,1024]{1,0:T(8,128)} custom-call(f32[128,1024]{1,0:T(8,128)S(1)} %shard_map.57.part), custom_call_target="tpu_custom_call" | custom-call | flops 10000000000 | bytes 262144 | tf_op jit(solution)/shard_map/pallas_call | solution.py:446
  441.0 27.8 %shard_map.59 = (f32[28,256,256]{2,1,0:T(8,128)}, f32[8,2,256,256]{3,2,1,0:T(8,128)}, f32[8,8,256]{2,1,0:T(8,128)}) custom-call(f32[1,1]{1,0:T(1,128)} %bitcast.26.refs_0_, f32[2,512,1024]{2,1,0:T(8,128)} %bitcast.46, f32[2,8,72,1024]{3,2,1,0:T(8,128)} %bitcast.40, ...), custom_call_target="tpu_custom_call", output_to_operand_aliasing={{0}: (4, {}), {1}: (5, {}), {2}: (6, {})} | custom-call | flops 40000000000 | bytes 8388608 | tf_op jit(solution)/shard_map/pallas_call | solution.py:279
  468.8 12.4 %shard_map.60.part = f32[128,1024]{1,0:T(8,128)S(1)} custom-call(s32[1]{0:T(128)} %bitcast.1.base, f32[4096,128]{1,0:T(8,128)S(1)} %collective-permute-done.3.got, f32[8192,1024]{1,0:T(8,128)} %refs_12_.1), custom_call_target="tpu_custom_call" | custom-call | flops 1073741824 | bytes 18874368 | tf_op jit(solution)/shard_map/pallas_call | solution.py:359
  481.2 8.7 %shard_map.61 = f32[16,1024]{1,0:T(8,128)} custom-call(f32[128,1024]{1,0:T(8,128)S(1)} %shard_map.60.part), custom_call_target="tpu_custom_call" | custom-call | flops 10000000000 | bytes 262144 | tf_op jit(solution)/shard_map/pallas_call | solution.py:446
  490.0 19.3 %shard_map.62 = (f32[28,256,256]{2,1,0:T(8,128)}, f32[8,2,256,256]{3,2,1,0:T(8,128)}, f32[8,8,256]{2,1,0:T(8,128)}) custom-call(f32[1,1]{1,0:T(1,128)} %bitcast.27.refs_0_, f32[2,512,1024]{2,1,0:T(8,128)} %bitcast.47, f32[2,8,72,1024]{3,2,1,0:T(8,128)} %bitcast.41, ...), custom_call_target="tpu_custom_call", output_to_operand_aliasing={{0}: (5, {}), {1}: (6, {}), {2}: (7, {})} | custom-call | flops 20000000000 | bytes 8388608 | tf_op jit(solution)/shard_map/pallas_call | solution.py:279
  509.3 6.9 %collective-permute-done.4.got = f32[4096,128]{1,0:T(8,128)} collective-permute-done((f32[4096,128]{1,0:T(8,128)}, f32[4096,128]{1,0:T(8,128)}, u32[]{:S(2)}, u32[]{:S(2)}) %collective-permute-start.4) | collective-permute-done | bytes 2097184 | tf_op jit(solution)/shard_map/ppermute | solution.py:488
  516.1 12.8 %shard_map.63.part = f32[128,1024]{1,0:T(8,128)S(1)} custom-call(s32[1]{0:T(128)} %bitcast.1.base, f32[4096,128]{1,0:T(8,128)} %collective-permute-done.4.got, f32[8192,1024]{1,0:T(8,128)} %refs_12_.1), custom_call_target="tpu_custom_call" | custom-call | flops 1073741824 | bytes 18874368 | tf_op jit(solution)/shard_map/pallas_call | solution.py:359
  535.9 22.5 %shard_map.65 = (f32[28,256,256]{2,1,0:T(8,128)}, f32[8,2,256,256]{3,2,1,0:T(8,128)}, f32[8,8,256]{2,1,0:T(8,128)}) custom-call(f32[1,1]{1,0:T(1,128)} %bitcast.28.refs_0_, f32[2,512,1024]{2,1,0:T(8,128)} %bitcast.48, f32[2,8,72,1024]{3,2,1,0:T(8,128)} %bitcast.42, ...), custom_call_target="tpu_custom_call", output_to_operand_aliasing={{0}: (6, {}), {1}: (7, {}), {2}: (8, {})} | custom-call | flops 20000000000 | bytes 8388608 | tf_op jit(solution)/shard_map/pallas_call | solution.py:279
  564.5 12.8 %shard_map.66.part = f32[128,1024]{1,0:T(8,128)S(1)} custom-call(s32[1]{0:T(128)} %bitcast.1.base, f32[4096,128]{1,0:T(8,128)} %collective-permute-done.5.got, f32[8192,1024]{1,0:T(8,128)} %refs_12_.1), custom_call_target="tpu_custom_call" | custom-call | flops 1073741824 | bytes 18874368 | tf_op jit(solution)/shard_map/pallas_call | solution.py:359
  577.3 7.5 %shard_map.67 = f32[16,1024]{1,0:T(8,128)} custom-call(f32[128,1024]{1,0:T(8,128)S(1)} %shard_map.66.part), custom_call_target="tpu_custom_call" | custom-call | flops 10000000000 | bytes 262144 | tf_op jit(solution)/shard_map/pallas_call | solution.py:446
  584.8 26.2 %shard_map.68 = (f32[28,256,256]{2,1,0:T(8,128)}, f32[8,2,256,256]{3,2,1,0:T(8,128)}, f32[8,8,256]{2,1,0:T(8,128)}) custom-call(f32[1,1]{1,0:T(1,128)} %bitcast.29.refs_0_, f32[2,512,1024]{2,1,0:T(8,128)} %bitcast.49, f32[2,8,72,1024]{3,2,1,0:T(8,128)} %bitcast.43, ...), custom_call_target="tpu_custom_call", output_to_operand_aliasing={{0}: (7, {}), {1}: (8, {}), {2}: (9, {})} | custom-call | flops 20000000000 | bytes 8388608 | tf_op jit(solution)/shard_map/pallas_call | solution.py:279
  611.9 35.7 %shard_map.69 = (f32[28,256,256]{2,1,0:T(8,128)}, f32[8,2,256,256]{3,2,1,0:T(8,128)}, f32[8,8,256]{2,1,0:T(8,128)}, f32[2,1024]{1,0:T(2,128)}, f32[64,128]{1,0:T(8,128)}) custom-call(f32[1,1]{1,0:T(1,128)} %bitcast.30.refs_0_, f32[2,512,1024]{2,1,0:T(8,128)} %bitcast.50, ...), custom_call_target="tpu_custom_call", output_to_operand_aliasing={{0}: (8, {}), {1}: (9, {}), {2}: (10, {})} | custom-call | flops 20000000000 | bytes 8388608 | tf_op jit(solution)/shard_map/pallas_call | solution.py:279
  (50 shorter events, 50.1 us)
Async XLA Ops:
  7.2 101.3 %reduce-scatter.2.cloned.1.call-start = ((), (), s32[]{:S(2)}) async-start(), calls=%async_computation.1 | async-start | bytes 2359296 | tf_op jit(solution)/shard_map/reduce_scatter | solution.py:478
  70.0 328.0 %all-gather.8.cloned.1.call-start = ((), (), s32[]{:S(2)}) async-start(), calls=%async_computation.2 | async-start | bytes 4456448 | tf_op jit(solution)/shard_map/all_gather | solution.py:481
  108.5 289.6 %all-gather.10.cloned.1.call-start = ((), (), s32[]{:S(2)}) async-start(), calls=%async_computation.3 | async-start | bytes 5013504 | tf_op jit(solution)/shard_map/all_gather | solution.py:481
  113.0 105.6 %collective-permute-start = (f32[4096,256]{1,0:T(8,128)}, f32[4096,256]{1,0:T(8,128)}, u32[]{:S(2)}, u32[]{:S(2)}) collective-permute-start(f32[4096,256]{1,0:T(8,128)} %constant_dynamic-slice_fusion.5), channel_id=1, source_target_pairs={{0,8},{8,0},{1,9},{9,1},{2,10},{10,2},{3,11},{11,3},{4,12},{12,4},... | collective-permute-start | bytes 12582920 | tf_op jit(solution)/shard_map/ppermute | solution.py:488
  114.5 33.9 %copy-start = (f32[8192]{0:T(1024)S(1)}, f32[8192]{0:T(1024)}, u32[]{:S(2)}) copy-start(f32[8192]{0:T(1024)} %param.4) | copy-start | bytes 98308
  256.0 184.9 %all-gather.12.cloned.1.call-start = ((), (), s32[]{:S(2)}) async-start(), calls=%async_computation.4 | async-start | bytes 2228224 | tf_op jit(solution)/shard_map/all_gather | solution.py:481
  260.6 108.5 %collective-permute-start.1 = (f32[4096,256]{1,0:T(8,128)}, f32[4096,256]{1,0:T(8,128)}, u32[]{:S(2)}, u32[]{:S(2)}) collective-permute-start(f32[4096,256]{1,0:T(8,128)} %constant_dynamic-slice_fusion.4), channel_id=1, source_target_pairs={{0,8},{8,0},{1,9},{9,1},{2,10},{10,2},{3,11},{11,3},{4,12},{12,4},... | collective-permute-start | bytes 12582920 | tf_op jit(solution)/shard_map/ppermute | solution.py:488
  265.2 153.6 %collective-permute-start.2 = (f32[4096,128]{1,0:T(8,128)}, f32[4096,128]{1,0:T(8,128)}, u32[]{:S(2)}, u32[]{:S(2)}) collective-permute-start(f32[4096,128]{1,0:T(8,128)} %constant_dynamic-slice_fusion.3), channel_id=1, source_target_pairs={{0,8},{8,0},{1,9},{9,1},{2,10},{10,2},{3,11},{11,3},{4,12},{12,4},... | collective-permute-start | bytes 6291464 | tf_op jit(solution)/shard_map/ppermute | solution.py:488
  268.8 199.9 %collective-permute-start.3 = (f32[4096,128]{1,0:T(8,128)}, f32[4096,128]{1,0:T(8,128)S(1)}, u32[]{:S(2)}, u32[]{:S(2)}) collective-permute-start(f32[4096,128]{1,0:T(8,128)} %constant_dynamic-slice_fusion.2), channel_id=1, source_target_pairs={{0,8},{8,0},{1,9},{9,1},{2,10},{10,2},{3,11},{11,3},{4,12},{12,4},... | collective-permute-start | bytes 6291464 | tf_op jit(solution)/shard_map/ppermute | solution.py:488
  273.4 242.8 %collective-permute-start.4 = (f32[4096,128]{1,0:T(8,128)}, f32[4096,128]{1,0:T(8,128)}, u32[]{:S(2)}, u32[]{:S(2)}) collective-permute-start(f32[4096,128]{1,0:T(8,128)} %constant_dynamic-slice_fusion.1), channel_id=1, source_target_pairs={{0,8},{8,0},{1,9},{9,1},{2,10},{10,2},{3,11},{11,3},{4,12},{12,4},... | collective-permute-start | bytes 6291464 | tf_op jit(solution)/shard_map/ppermute | solution.py:488
  277.0 287.5 %collective-permute-start.5 = (f32[4096,128]{1,0:T(8,128)}, f32[4096,128]{1,0:T(8,128)}, u32[]{:S(2)}, u32[]{:S(2)}) collective-permute-start(f32[4096,128]{1,0:T(8,128)} %constant_dynamic-slice_fusion), channel_id=1, source_target_pairs={{0,8},{8,0},{1,9},{9,1},{2,10},{10,2},{3,11},{11,3},{4,12},{12,4},... | collective-permute-start | bytes 6291464 | tf_op jit(solution)/shard_map/ppermute | solution.py:488
  397.8 92.2 %all-gather.14.cloned.1.call-start = ((), (), s32[]{:S(2)}) async-start(), calls=%async_computation.5 | async-start | bytes 1114112 | tf_op jit(solution)/shard_map/all_gather | solution.py:481
  440.9 95.0 %all-gather.16.cloned.1.call-start = ((), (), s32[]{:S(2)}) async-start(), calls=%async_computation.6 | async-start | bytes 1114112 | tf_op jit(solution)/shard_map/all_gather | solution.py:481
  489.9 94.9 %all-gather.18.cloned.1.call-start = ((), (), s32[]{:S(2)}) async-start(), calls=%async_computation.7 | async-start | bytes 1114112 | tf_op jit(solution)/shard_map/all_gather | solution.py:481
  535.6 76.3 %all-gather.20.cloned.1.call-start = ((), (), s32[]{:S(2)}) async-start(), calls=%async_computation.8 | async-start | bytes 1114112 | tf_op jit(solution)/shard_map/all_gather | solution.py:481
  611.9 39.8 %copy-start.1 = (f32[8192]{0:T(1024)S(1)}, f32[8192]{0:T(1024)}, u32[]{:S(2)}) copy-start(f32[8192]{0:T(1024)} %param.4) | copy-start | bytes 98308
  647.5 4.2 collective-permute-start.6
Sparse Core Ops, SparseCore 0:
  70.2 38.2 reduce-scatter.1
  110.7 48.7 all-gather.7
  256.1 52.0 all-gather.9
  397.9 36.8 all-gather.11
  441.0 29.7 all-gather.13
  490.0 29.4 all-gather.15
  535.7 29.8 all-gather.17
  584.9 26.9 all-gather.19
